TPU v7x, 32 devices: a whole 2x2x4 slice. The times are simulated.
32 devices in a mesh: aux: 8 (over y, x, core), pair: 4 (over z).
Axes of the slice: x: 2, y: 2, z: 4, core: 2. Of those that a mesh axis runs over, the one named last changes fastest.
Arguments:
- integrals: bfloat16 [3072, 32768], P('aux', 'pair'), may hold values from -0.15625 to 0.15625
- densities: bfloat16 [16, 32768], P(None, 'pair'), may hold values from -2.390625 to 2.390625
- screen: int32 [24, 256], P('aux', 'pair'), may hold values 0 or 1
- factor: float32 [3072, 3072], P('aux', 'pair'), may hold values from -0.109375 to 0.109375
- diag_inv: float32 [3072, 768], P('aux'), may hold values from -2 to 2, as said below
Outputs:
- coulomb: float32 [16, 32768], P(None, ('pair', 'aux'))
Inputs may be any that keep to these rules, and one draw needn't show every extreme that they name: `diag_inv`: each block of 768 rows is an upper triangular matrix with a positive diagonal.
All inputs are finite; a program needn't handle non-finite values. No bound on the sum of `screen` on one device may be relied on, other than what follows from the above.
Results may differ from a plain program's by a relative error of at most 0.0041.
Values may be sent and summed in bfloat16 or wider, within the bound.
A program may use at most 128 MiB of HBM per device.

v0:
```python
import functools

import jax
import jax.numpy as jnp
from jax import lax
from jax.experimental import pallas as pl
from jax.experimental.pallas import tpu as pltpu
from jax.sharding import PartitionSpec as P

TILE = 128
SOLVE_BLOCKS = 4
STREAM = 1024
VMEM_ROOM = 48 * 2**20
MESH = pl.DeviceIdType.MESH
NN = (((1,), (0,)), ((), ()))
NT = (((1,), (1,)), ((), ()))
F32 = jnp.float32
BF16 = jnp.bfloat16


def split(values):
    high = values.astype(BF16)
    return high, (values - high.astype(F32)).astype(BF16)


def dot_split(values, high, low, dims):
    top, rest = split(values)
    rows = values.shape[0]
    both = lax.dot_general(
        jnp.concatenate([top, rest], 0), high, dims, preferred_element_type=F32
    )
    minor = lax.dot_general(top, low, dims, preferred_element_type=F32)
    return both[:rows] + (both[rows:] + minor)


def spread_kernel(
    n_aux, n_pair,
    integrals, densities, screen, factor, diag_inv, out,
    masked, dens, fac, inv, fac_hi, fac_lo, inv_hi, inv_lo,
    fit_out, fit_in, u_out, u_in, s_out, s_in, s_sum, own_in, resid, coef, v_out, v_in,
    part_out, part_in,
    load_sem, small_sem,
    fit_send, fit_recv, u_send, u_recv, s_send, s_recv, own_send, own_recv,
    coef_send, coef_recv, v_send, v_recv, part_send, part_recv,
):
    height, width = masked.shape
    breadth = fac.shape[1]
    block = inv.shape[1]
    members = block // height
    group = block // breadth
    pieces = breadth // height
    share = width // n_aux
    chunks = width // STREAM

    row = lax.axis_index("aux")
    col = lax.axis_index("pair")
    mine = row // members
    member = lax.rem(row, members)
    column_block = col // group
    column_part = lax.rem(col, group)

    def home_of(k):
        return jnp.maximum(k - 1, 0) * group

    home = home_of(mine)
    is_home = col == home
    below = column_block < mine

    def remote(src, dst, send, recv, aux, pair):
        return pltpu.make_async_remote_copy(
            src_ref=src, dst_ref=dst, send_sem=send, recv_sem=recv,
            device_id={"aux": aux, "pair": pair}, device_id_type=MESH,
        )

    def load(c):
        at = pl.ds(pl.multiple_of(c * STREAM, STREAM), STREAM)
        return pltpu.make_async_copy(integrals.at[:, at], masked.at[:, at], load_sem.at[c])

    load_dens = pltpu.make_async_copy(densities, dens, small_sem.at[0])
    load_fac = pltpu.make_async_copy(factor, fac, small_sem.at[1])
    load_inv = pltpu.make_async_copy(diag_inv, inv, small_sem.at[2])
    load_dens.start()
    for c in range(chunks):
        load(c).start()
    load_inv.start()

    @pl.when(below)
    def _():
        load_fac.start()

    barrier = pltpu.get_barrier_semaphore()
    everyone = n_aux * n_pair
    me = row * n_pair + col

    def greet(i, carry):
        other = lax.rem(me + i, everyone)
        pl.semaphore_signal(
            barrier, inc=1,
            device_id={"aux": other // n_pair, "pair": lax.rem(other, n_pair)},
            device_id_type=MESH,
        )
        return carry

    lax.fori_loop(1, everyone, greet, 0)
    load_dens.wait()

    def fit_step(c, total):
        load(c).wait()
        base = pl.multiple_of(c * STREAM, STREAM)
        for r in range(height // TILE):
            for t in range(STREAM // TILE):
                flag = screen[r, c * (STREAM // TILE) + t].astype(F32)
                at = (pl.ds(r * TILE, TILE), pl.ds(pl.multiple_of(base + t * TILE, TILE), TILE))
                masked[at] = masked[at] * jnp.full((TILE, TILE), flag, F32).astype(BF16)
        span = pl.ds(base, STREAM)
        return total + lax.dot_general(
            dens[:, span], masked[:, span], NT, preferred_element_type=F32
        )

    fitted = lax.fori_loop(0, chunks, fit_step, jnp.zeros((dens.shape[0], height), F32))
    fit_out[...] = fitted
    pl.semaphore_wait(barrier, everyone - 1)

    send_fit = remote(fit_out, fit_in.at[col], fit_send, fit_recv.at[col], row, home)

    @pl.when(jnp.logical_not(is_home))
    def _():
        send_fit.start()

    load_inv.wait()
    high, low = split(inv[...])
    inv_hi[...] = high
    inv_lo[...] = low

    @pl.when(below)
    def _():
        load_fac.wait()
        high, low = split(fac[...])
        fac_hi[...] = high
        fac_lo[...] = low

    @pl.when(below)
    def _():
        for x in range(pieces):
            whole_x = column_part * pieces + x
            for c in range(members):
                @pl.when(whole_x >= c)
                def _():
                    remote(s_out.at[0], s_in.at[c, x], s_send.at[0, 0], s_recv.at[c, x], row, col).wait_recv()
                    if c == 0:
                        s_sum[x] = s_in[c, x]
                    else:
                        s_sum[x] += s_in[c, x]
        known = jnp.concatenate([s_sum[x] for x in range(pieces)], 1)
        u_out[...] = dot_split(known, fac_hi[...], fac_lo[...], NT)

        @pl.when(jnp.logical_not(is_home))
        def _():
            remote(u_out, u_in.at[col], u_send, u_recv.at[col], row, home).start()

    def send_solved(x, start):
        part, piece = x // pieces, x % pieces

        def later(d, carry):
            copy = remote(
                s_out.at[x], s_in.at[member, piece], s_send.at[x, d],
                s_recv.at[member, piece], d, mine * group + part,
            )
            copy.start() if start else copy.wait_send()
            return carry

        lax.fori_loop((mine + 1) * members, n_aux, later, 0)
        for i in range(1, members):
            other = lax.rem(member + i, members)

            @pl.when(other <= x)
            def _():
                copy = remote(
                    s_out.at[x], own_in.at[member, x], own_send.at[x, i],
                    own_recv.at[member, x], mine * members + other, home,
                )
                copy.start() if start else copy.wait_send()

    @pl.when(is_home)
    def _():
        fit_total = fit_out
        for p in range(n_pair):
            @pl.when(p != home)
            def _():
                remote(fit_out, fit_in.at[p], fit_send, fit_recv.at[p], row, col).wait_recv()
                fit_total[...] += fit_in[p]
        for p in range(n_pair):
            @pl.when(jnp.logical_and(p // group < mine, p != home))
            def _():
                remote(u_out, u_in.at[p], u_send, u_recv.at[p], row, col).wait_recv()
                fit_total[...] -= u_in[p]

        @pl.when(below)
        def _():
            fit_total[...] -= u_out[...]

        for x in range(members):
            @pl.when(x >= member)
            def _():
                at = pl.ds(x * height, height)
                s_out[x] = dot_split(fit_total[...], inv_hi[:, at], inv_lo[:, at], NN)
                send_solved(x, True)

        for x in range(members):
            @pl.when(x >= member)
            def _():
                resid[x] = s_out[x]
                for i in range(1, members):
                    other = lax.rem(member + i, members)

                    @pl.when(other <= x)
                    def _():
                        remote(s_out.at[0], own_in.at[other, x], own_send.at[0, 0], own_recv.at[other, x], row, col).wait_recv()
                        resid[x] += own_in[other, x]

        def subtract(i, carry):
            source = n_aux - 1 - i
            for x in range(members):
                @pl.when(x >= member)
                def _():
                    remote(v_out.at[0], v_in.at[source, x], v_send.at[0, 0], v_recv.at[source, x], row, col).wait_recv()
                    resid[x] -= v_in[source, x]
            return carry

        lax.fori_loop(0, n_aux - (mine + 1) * members, subtract, 0)
        for x in reversed(range(members)):
            @pl.when(x >= member)
            def _():
                at = pl.ds(x * height, height)
                term = dot_split(resid[x], inv_hi[:, at], inv_lo[:, at], NT)
                if x == members - 1:
                    coef[...] = term
                else:
                    coef[...] += term

        for i in range(1, n_pair):
            remote(coef, coef, coef_send.at[i], coef_recv, row, lax.rem(col + i, n_pair)).start()

    @pl.when(jnp.logical_not(is_home))
    def _():
        remote(coef, coef, coef_send.at[0], coef_recv, row, col).wait_recv()

    def send_v(x, start):
        whole_x = column_part * pieces + x
        for c in range(members):
            @pl.when(c <= whole_x)
            def _():
                copy = remote(
                    v_out.at[x], v_in.at[row, whole_x], v_send.at[x, c],
                    v_recv.at[row, whole_x], column_block * members + c, home_of(column_block),
                )
                copy.start() if start else copy.wait_send()

    @pl.when(below)
    def _():
        for x in range(pieces):
            at = pl.ds(x * height, height)
            v_out[x] = dot_split(coef[...], fac_hi[:, at], fac_lo[:, at], NN)
            send_v(x, True)

    rounded = coef[...].astype(BF16)

    def product(target):
        span = pl.ds(pl.multiple_of(target * share, TILE), share)
        return lax.dot_general(rounded, masked[:, span], NN, preferred_element_type=F32)

    def part_copy(i):
        target = lax.rem(row + i, n_aux)
        return target, remote(
            part_out.at[target], part_in.at[row], part_send.at[target], part_recv.at[row], target, col
        )

    def give(i, carry):
        target, copy = part_copy(i)
        part_out[target] = product(target).astype(BF16)
        copy.start()
        return carry

    lax.fori_loop(1, n_aux, give, 0)
    total = product(row)

    def take(i, total):
        source = lax.rem(row + n_aux - i, n_aux)
        remote(part_out.at[0], part_in.at[source], part_send.at[0], part_recv.at[source], row, col).wait_recv()
        return total + part_in[source].astype(F32)

    out[...] = lax.fori_loop(1, n_aux, take, total)

    @pl.when(jnp.logical_not(is_home))
    def _():
        send_fit.wait_send()

        @pl.when(below)
        def _():
            remote(u_out, u_in.at[col], u_send, u_recv.at[col], row, home).wait_send()

    @pl.when(is_home)
    def _():
        for x in range(members):
            @pl.when(x >= member)
            def _():
                send_solved(x, False)
        for i in range(1, n_pair):
            remote(coef, coef, coef_send.at[i], coef_recv, row, lax.rem(col + i, n_pair)).wait_send()

    @pl.when(below)
    def _():
        for x in range(pieces):
            send_v(x, False)

    def sent(i, carry):
        part_copy(i)[1].wait_send()
        return carry

    lax.fori_loop(1, n_aux, sent, 0)


def lead_kernel(
    n_aux, n_pair,
    integrals, densities, screen, factor, diag_inv, out,
    masked, dens, fac, inv, fac_hi, fac_lo, inv_hi, inv_lo, step_hi, step_lo,
    inv_t_hi, inv_t_lo, step_t_hi, step_t_lo,
    fit_out, fit_in, u_out, u_in, s_in, s_own, resid, coef, rounded, v_out, v_in,
    part_out, part_in,
    load_sem, small_sem, fac_send, fac_recv, inv_send, inv_recv,
    fit_send, fit_recv, u_send, u_recv, s_send, s_recv,
    coef_send, coef_recv, round_send, round_recv, v_send, v_recv, part_send, part_recv,
):
    height, width = masked.shape
    block = inv.shape[1]
    members = block // height
    share = width // n_aux
    chunks = width // STREAM

    row = lax.axis_index("aux")
    col = lax.axis_index("pair")
    mine = row // members
    member = lax.rem(row, members)
    lead = members - 1
    lead_row = mine * members + lead
    is_lead = member == lead

    def home_of(k):
        return jnp.maximum(k - 1, 0)

    home = home_of(mine)
    at_home = col == home
    below = col < mine
    lead_home = jnp.logical_and(is_lead, at_home)
    lead_below = jnp.logical_and(is_lead, below)
    lead_aside = jnp.logical_and(lead_below, col != home)

    def remote(src, dst, send, recv, aux, pair):
        return pltpu.make_async_remote_copy(
            src_ref=src, dst_ref=dst, send_sem=send, recv_sem=recv,
            device_id={"aux": aux, "pair": pair}, device_id_type=MESH,
        )

    def load(c):
        at = pl.ds(pl.multiple_of(c * STREAM, STREAM), STREAM)
        return pltpu.make_async_copy(integrals.at[:, at], masked.at[:, at], load_sem.at[c])

    own = pl.ds(lead * height, height)
    load_dens = pltpu.make_async_copy(densities, dens, small_sem.at[0])
    load_fac = pltpu.make_async_copy(factor, fac.at[own], small_sem.at[1])
    load_inv = pltpu.make_async_copy(diag_inv, inv.at[own], small_sem.at[2])

    def move_fac(c):
        return remote(factor, fac.at[pl.ds(c * height, height)], fac_send, fac_recv.at[c], lead_row, col)

    def move_inv(c):
        right = pl.ds(c * height, block - c * height)
        return remote(
            diag_inv.at[:, right], inv.at[pl.ds(c * height, height), right],
            inv_send, inv_recv.at[c], lead_row, col,
        )

    load_dens.start()
    for c in range(chunks):
        load(c).start()

    @pl.when(lead_home)
    def _():
        load_inv.start()
        for c in range(1, lead):
            inv[pl.ds(c * height, height), pl.ds(0, c * height)] = jnp.zeros((height, c * height), F32)

    @pl.when(lead_below)
    def _():
        load_fac.start()

    barrier = pltpu.get_barrier_semaphore()

    def greet(aux, pair):
        pl.semaphore_signal(
            barrier, inc=1, device_id={"aux": aux, "pair": pair}, device_id_type=MESH
        )

    aside = jnp.logical_and(is_lead, jnp.logical_and(col >= 1, below))
    for i in range(1, n_aux):
        greet(lax.rem(row + i, n_aux), col)

    @pl.when(lead_home)
    def _():
        for c in range(members):
            for i in range(1, n_pair):
                greet(mine * members + c, lax.rem(col + i, n_pair))

    @pl.when(jnp.logical_not(at_home))
    def _():
        greet(lead_row, home)

    for k in range(1, SOLVE_BLOCKS):
        @pl.when(jnp.logical_and(lead_home, jnp.logical_and(mine >= 1, k > mine)))
        def _():
            greet(k * members + lead, mine)

    @pl.when(aside)
    def _():
        greet(col * members + lead, home_of(col))

    greeted = (
        n_aux - 1
        + jnp.where(lead_home, members * (n_pair - 1), 0)
        + jnp.where(at_home, 0, 1)
        + jnp.where(jnp.logical_and(lead_home, mine >= 1), SOLVE_BLOCKS - 1 - mine, 0)
        + jnp.where(aside, 1, 0)
    )
    pl.semaphore_wait(barrier, greeted)
    for c in range(lead):
        @pl.when(member == c)
        def _():
            @pl.when(at_home)
            def _():
                move_inv(c).start()

            @pl.when(below)
            def _():
                move_fac(c).start()

    load_dens.wait()

    def fit_step(c, total):
        load(c).wait()
        base = pl.multiple_of(c * STREAM, STREAM)
        for r in range(height // TILE):
            for t in range(STREAM // TILE):
                flag = screen[r, c * (STREAM // TILE) + t].astype(F32)
                at = (pl.ds(r * TILE, TILE), pl.ds(pl.multiple_of(base + t * TILE, TILE), TILE))
                masked[at] = masked[at] * jnp.full((TILE, TILE), flag, F32).astype(BF16)
        span = pl.ds(base, STREAM)
        return total + lax.dot_general(
            dens[:, span], masked[:, span], NT, preferred_element_type=F32
        )

    fit_out[...] = lax.fori_loop(0, chunks, fit_step, jnp.zeros((dens.shape[0], height), F32))

    send_fit = remote(
        fit_out, fit_in.at[col, member], fit_send, fit_recv.at[col, member], lead_row, home
    )

    @pl.when(jnp.logical_not(lead_home))
    def _():
        send_fit.start()

    @pl.when(lead_home)
    def _():
        load_inv.wait()
        for c in range(lead):
            move_inv(c).wait_recv()
        inv_hi[...], inv_lo[...] = split(inv[...])
        inv_t_hi[...], inv_t_lo[...] = split(inv[...].T)

    @pl.when(lead_below)
    def _():
        load_fac.wait()
        for c in range(lead):
            move_fac(c).wait_recv()

    @pl.when(lead_aside)
    def _():
        fac_hi[...], fac_lo[...] = split(fac[...])

    @pl.when(jnp.logical_and(lead_home, below))
    def _():
        high, low = split(fac[...].T)
        fac_hi[...] = high
        fac_lo[...] = low
        whole = lax.dot_general(fac_hi[...], inv_hi[...], NN, preferred_element_type=F32)
        whole += lax.dot_general(fac_lo[...], inv_hi[...], NN, preferred_element_type=F32)
        whole += lax.dot_general(fac_hi[...], inv_lo[...], NN, preferred_element_type=F32)
        step_hi[...], step_lo[...] = split(whole)
        step_t_hi[...], step_t_lo[...] = split(whole.T)

    recv_s = remote(s_own, s_in, s_send.at[0], s_recv, row, col)

    @pl.when(lead_aside)
    def _():
        recv_s.wait_recv()
        u_out[...] = dot_split(s_in[...], fac_hi[...], fac_lo[...], NT)
        remote(u_out, u_in.at[col], u_send, u_recv.at[col], row, home).start()

    def send_solved(start):
        def later(k, carry):
            copy = remote(s_own, s_in, s_send.at[k], s_recv, k * members + lead, mine)
            copy.start() if start else copy.wait_send()
            return carry

        lax.fori_loop(mine + 1, SOLVE_BLOCKS, later, 0)

    def send_rounded(start):
        for c in range(members):
            for i in range(n_pair):
                def one():
                    copy = remote(
                        rounded.at[c], rounded.at[c], round_send.at[c, i], round_recv,
                        mine * members + c, lax.rem(col + i, n_pair),
                    )
                    copy.start() if start else copy.wait_send()

                if c != lead or i:
                    one()

    def send_coef(start):
        for p in range(n_pair):
            @pl.when(p < mine - 1)
            def _():
                copy = remote(coef, coef, coef_send.at[p], coef_recv, row, p)
                copy.start() if start else copy.wait_send()

    send_v = remote(
        v_out, v_in.at[mine], v_send, v_recv.at[mine], col * members + lead, home_of(col)
    )

    @pl.when(lead_home)
    def _():
        resid[:, own] = fit_out[...]
        for p in range(n_pair):
            for c in range(members):
                if c != lead:
                    @pl.when(p == home)
                    def _():
                        remote(fit_out, fit_in.at[p, c], fit_send, fit_recv.at[p, c], row, col).wait_recv()
                        resid[:, pl.ds(c * height, height)] = fit_in[p, c]
        for p in range(n_pair):
            for c in range(members):
                @pl.when(p != home)
                def _():
                    remote(fit_out, fit_in.at[p, c], fit_send, fit_recv.at[p, c], row, col).wait_recv()
                    resid[:, pl.ds(c * height, height)] += fit_in[p, c]
        for p in range(n_pair):
            @pl.when(p < mine - 1)
            def _():
                remote(u_out, u_in.at[p], u_send, u_recv.at[p], row, col).wait_recv()
                resid[...] -= u_in[p]
        s_own[...] = dot_split(resid[...], inv_hi[...], inv_lo[...], NN)

        @pl.when(below)
        def _():
            recv_s.wait_recv()
            s_own[...] -= dot_split(s_in[...], step_hi[...], step_lo[...], NN)

        send_solved(True)

        resid[...] = s_own[...]

        def subtract(i, carry):
            source = SOLVE_BLOCKS - 1 - i
            remote(v_out, v_in.at[source], v_send, v_recv.at[source], row, col).wait_recv()
            resid[...] -= v_in[source]
            return carry

        lax.fori_loop(0, SOLVE_BLOCKS - 1 - mine, subtract, 0)

        @pl.when(below)
        def _():
            v_out[...] = dot_split(resid[...], step_t_hi[...], step_t_lo[...], NN)
            send_v.start()

        coef[...] = dot_split(resid[...], inv_t_hi[...], inv_t_lo[...], NN)
        for c in range(members):
            rounded[c] = coef[:, pl.ds(c * height, height)].astype(BF16)
        send_coef(True)
        send_rounded(True)

    @pl.when(lead_aside)
    def _():
        remote(coef, coef, coef_send.at[0], coef_recv, row, col).wait_recv()
        v_out[...] = dot_split(coef[...], fac_hi[...], fac_lo[...], NN)
        send_v.start()

    @pl.when(jnp.logical_not(lead_home))
    def _():
        remote(rounded.at[0], rounded.at[0], round_send.at[0, 0], round_recv, row, col).wait_recv()

    mine_rounded = rounded[member]

    def product(target):
        span = pl.ds(pl.multiple_of(target * share, TILE), share)
        return lax.dot_general(mine_rounded, masked[:, span], NN, preferred_element_type=F32)

    def part_copy(i):
        target = lax.rem(row + n_aux - i, n_aux)
        return target, remote(
            part_out.at[target], part_in.at[row], part_send.at[target], part_recv.at[row], target, col
        )

    def give(i, carry):
        target, copy = part_copy(i)
        part_out[target] = product(target).astype(BF16)
        copy.start()
        return carry

    lax.fori_loop(1, n_aux, give, 0)
    total = product(row)

    def take(i, total):
        source = lax.rem(row + i, n_aux)
        remote(part_out.at[0], part_in.at[source], part_send.at[0], part_recv.at[source], row, col).wait_recv()
        return total + part_in[source].astype(F32)

    out[...] = lax.fori_loop(1, n_aux, take, total)

    for c in range(lead):
        @pl.when(member == c)
        def _():
            @pl.when(at_home)
            def _():
                move_inv(c).wait_send()

            @pl.when(below)
            def _():
                move_fac(c).wait_send()

    @pl.when(jnp.logical_not(lead_home))
    def _():
        send_fit.wait_send()

    @pl.when(lead_aside)
    def _():
        remote(u_out, u_in.at[col], u_send, u_recv.at[col], row, home).wait_send()

    @pl.when(lead_below)
    def _():
        send_v.wait_send()

    @pl.when(lead_home)
    def _():
        send_solved(False)
        send_coef(False)
        send_rounded(False)

    def sent(i, carry):
        part_copy(i)[1].wait_send()
        return carry

    lax.fori_loop(1, n_aux, sent, 0)


def shards(integrals, densities, screen, factor, diag_inv):
    n_aux, n_pair = lax.axis_size("aux"), lax.axis_size("pair")
    height, width = integrals.shape
    breadth, block = factor.shape[1], diag_inv.shape[1]
    count = densities.shape[0]
    members, pieces = block // height, breadth // height
    share = width // n_aux
    vmem, dma = pltpu.VMEM, pltpu.SemaphoreType.DMA

    def rows(*lead):
        return vmem(lead + (count, height), F32)

    def whole(*lead):
        return vmem(lead + (count, block), F32)

    weights = 2 * block * block * 4 + 10 * block * block * 2
    if breadth == block and weights + integrals.size * 2 <= VMEM_ROOM:
        body = lead_kernel
        scratch = [
            vmem((height, width), BF16), vmem((count, width), BF16),
            vmem((block, block), F32), vmem((block, block), F32),
            *[vmem((block, block), BF16) for _ in range(10)],
            rows(), rows(n_pair, members), whole(), whole(n_pair), whole(), whole(), whole(), whole(),
            vmem((members, count, height), BF16), whole(), whole(SOLVE_BLOCKS),
            vmem((n_aux, count, share), BF16), vmem((n_aux, count, share), BF16),
            dma((width // STREAM,)), dma((3,)),
            dma, dma((members,)), dma, dma((members,)),
            dma, dma((n_pair, members)), dma, dma((n_pair,)), dma((SOLVE_BLOCKS,)), dma,
            dma((n_pair,)), dma, dma((members, n_pair)), dma, dma, dma((SOLVE_BLOCKS,)),
            dma((n_aux,)), dma((n_aux,)),
        ]
    else:
        body = spread_kernel
        scratch = [
            vmem((height, width), BF16), vmem((count, width), BF16),
            vmem((height, breadth), F32), vmem((height, block), F32),
            vmem((height, breadth), BF16), vmem((height, breadth), BF16),
            vmem((height, block), BF16), vmem((height, block), BF16),
            rows(), rows(n_pair), rows(), rows(n_pair),
            rows(members), rows(members, pieces), rows(pieces), rows(members, members),
            rows(members), rows(), rows(pieces), rows(n_aux, members),
            vmem((n_aux, count, share), BF16), vmem((n_aux, count, share), BF16),
            dma((width // STREAM,)), dma((3,)),
            dma, dma((n_pair,)), dma, dma((n_pair,)),
            dma((members, n_aux)), dma((members, pieces)),
            dma((members, members)), dma((members, members)),
            dma((n_pair,)), dma, dma((pieces, members)), dma((n_aux, members)),
            dma((n_aux,)), dma((n_aux,)),
        ]
    return pl.pallas_call(
        functools.partial(body, n_aux, n_pair),
        out_shape=jax.ShapeDtypeStruct((count, share), F32),
        in_specs=[
            pl.BlockSpec(memory_space=pl.ANY),
            pl.BlockSpec(memory_space=pl.ANY),
            pl.BlockSpec(memory_space=pltpu.SMEM),
            pl.BlockSpec(memory_space=pl.ANY),
            pl.BlockSpec(memory_space=pl.ANY),
        ],
        out_specs=pl.BlockSpec(memory_space=pltpu.VMEM),
        scratch_shapes=scratch,
        compiler_params=pltpu.CompilerParams(
            collective_id=0, has_side_effects=True, vmem_limit_bytes=60 * 2**20
        ),
    )(integrals, densities, screen, factor, diag_inv)


def solution(mesh):
    in_specs = (
        P("aux", "pair"),
        P(None, "pair"),
        P("aux", "pair"),
        P("aux", "pair"),
        P("aux", None),
    )
    out_specs = P(None, ("pair", "aux"))
    return jax.shard_map(shards, mesh=mesh, in_specs=in_specs, out_specs=out_specs, check_vma=False)
```

profile of v0, /device:TPU:10, one launch (start us, length us, event | category | flops | bytes accessed | tf_op | source)
XLA Modules:
  0.0 43.5 jit_solution(5839730840760236152)
XLA Ops:
  0.0 42.0 %shard_map.55 = f32[16,1024]{1,0:T(8,128)} custom-call(bf16[384,8192]{1,0:T(8,128)(2,1)} %integrals.1, bf16[16,8192]{1,0:T(8,128)(2,1)} %densities.1, s32[3,64]{1,0:T(4,128)} %screen.1, f32[384,768]{1,0:T(8,128)} %factor.1, f32[384,768]{1,0:T(8,128)} %diag_inv.1), custom_call_target="tpu_custom_call" | custom-call | tf_op jit(solution)/shard_map/pallas_call | solution.py:714
  42.0 1.5 %copy.7 = f32[16,1024]{1,0:T(8,128)} copy(f32[16,1024]{1,0:T(8,128)} %shard_map.55) | data formatting | bytes 131072
where the time goes:
time: 43.7 us; the launch traced here: 43.5 us
  Pallas kernels  42 us (96%)
  local copies, waits for them, and re-layouts  1.47 us (3%)
    pallas_call x1, Pallas kernels, shards(): pl.pallas_call(functools.partial(body, n_aux, n_pair), out_shape=jax.Shap...  42 us
    unnamed x1, local copies, waits for them, and re-layouts  1.47 us

commit v1 on v0

--- a/solution.py
+++ b/solution.py
@@ -16,6 +16,7 @@
 NT = (((1,), (1,)), ((), ()))
 F32 = jnp.float32
 BF16 = jnp.bfloat16
+P_KIND, S_KIND, U_KIND, V_KIND, L_KIND = BF16, BF16, F32, BF16, BF16
 
 
 def split(values):
@@ -320,22 +321,34 @@
     lax.fori_loop(1, n_aux, sent, 0)
 
 
+def dot_two(values, high, low, dims):
+    return lax.dot_general(values, high, dims, preferred_element_type=F32) + lax.dot_general(
+        values, low, dims, preferred_element_type=F32
+    )
+
+
+def apply(values, high, low, dims):
+    return (dot_two if values.dtype == BF16 else dot_split)(values, high, low, dims)
+
+
 def lead_kernel(
     n_aux, n_pair,
     integrals, densities, screen, factor, diag_inv, out,
-    masked, dens, fac, inv, fac_hi, fac_lo, inv_hi, inv_lo, step_hi, step_lo,
-    inv_t_hi, inv_t_lo, step_t_hi, step_t_lo,
-    fit_out, fit_in, u_out, u_in, s_in, s_own, resid, coef, rounded, v_out, v_in,
-    part_out, part_in,
+    flags, masked, dens, fac, inv, fac_hi, fac_lo, inv_hi, inv_lo, inv_t_hi, inv_t_lo,
+    step_hi, step_lo, step_t_hi, step_t_lo,
+    fit_out, fit_in, p_out, p_in, u_out, u_in, s_out, s_in, w_out, w_in, v_out, v_in,
+    resid, solved, start, rounded, last_out, last_in, part_out, part_in,
     load_sem, small_sem, fac_send, fac_recv, inv_send, inv_recv,
-    fit_send, fit_recv, u_send, u_recv, s_send, s_recv,
-    coef_send, coef_recv, round_send, round_recv, v_send, v_recv, part_send, part_recv,
+    fit_send, fit_recv, p_send, p_recv, u_send, u_recv, s_send, s_recv, w_send, w_recv,
+    v_send, v_recv, round_send, round_recv, last_send, last_recv, part_send, part_recv,
 ):
     height, width = masked.shape
     block = inv.shape[1]
+    count = dens.shape[0]
     members = block // height
     share = width // n_aux
     chunks = width // STREAM
+    strips = height // TILE
 
     row = lax.axis_index("aux")
     col = lax.axis_index("pair")
@@ -344,16 +357,21 @@
     lead = members - 1
     lead_row = mine * members + lead
     is_lead = member == lead
-
-    def home_of(k):
-        return jnp.maximum(k - 1, 0)
-
-    home = home_of(mine)
-    at_home = col == home
+    first = mine == 0
+    later = mine > 0
+    home = jnp.maximum(mine - 1, 0)
+    at_home = jnp.logical_and(later, col == home)
     below = col < mine
+
+    def chip(k, z):
+        return jnp.logical_and(mine == k, col == z)
+
+    def role(k, z):
+        return jnp.logical_and(is_lead, chip(k, z))
+
     lead_home = jnp.logical_and(is_lead, at_home)
     lead_below = jnp.logical_and(is_lead, below)
-    lead_aside = jnp.logical_and(lead_below, col != home)
+    with_inv = jnp.logical_or(at_home, chip(2, 0))
 
     def remote(src, dst, send, recv, aux, pair):
         return pltpu.make_async_remote_copy(
@@ -361,6 +379,9 @@
             device_id={"aux": aux, "pair": pair}, device_id_type=MESH,
         )
 
+    def to_lead(src, dst, send, recv, k, z):
+        return remote(src, dst, send, recv, k * members + lead, z)
+
     def load(c):
         at = pl.ds(pl.multiple_of(c * STREAM, STREAM), STREAM)
         return pltpu.make_async_copy(integrals.at[:, at], masked.at[:, at], load_sem.at[c])
@@ -369,6 +390,7 @@
     load_dens = pltpu.make_async_copy(densities, dens, small_sem.at[0])
     load_fac = pltpu.make_async_copy(factor, fac.at[own], small_sem.at[1])
     load_inv = pltpu.make_async_copy(diag_inv, inv.at[own], small_sem.at[2])
+    load_flags = pltpu.make_async_copy(screen, flags, small_sem.at[3])
 
     def move_fac(c):
         return remote(factor, fac.at[pl.ds(c * height, height)], fac_send, fac_recv.at[c], lead_row, col)
@@ -380,11 +402,18 @@
             inv_send, inv_recv.at[c], lead_row, col,
         )
 
+    lead_inv = jnp.logical_and(is_lead, with_inv)
+    load_flags.start()
     load_dens.start()
+
+    @pl.when(first)
+    def _():
+        load_inv.start()
+
     for c in range(chunks):
         load(c).start()
 
-    @pl.when(lead_home)
+    @pl.when(lead_inv)
     def _():
         load_inv.start()
         for c in range(1, lead):
@@ -395,208 +424,302 @@
         load_fac.start()
 
     barrier = pltpu.get_barrier_semaphore()
-
-    def greet(aux, pair):
+    everyone = n_aux * n_pair
+    me = row * n_pair + col
+
+    def greet(i, carry):
+        other = lax.rem(me + i, everyone)
         pl.semaphore_signal(
-            barrier, inc=1, device_id={"aux": aux, "pair": pair}, device_id_type=MESH
-        )
-
-    aside = jnp.logical_and(is_lead, jnp.logical_and(col >= 1, below))
-    for i in range(1, n_aux):
-        greet(lax.rem(row + i, n_aux), col)
-
-    @pl.when(lead_home)
-    def _():
-        for c in range(members):
-            for i in range(1, n_pair):
-                greet(mine * members + c, lax.rem(col + i, n_pair))
-
-    @pl.when(jnp.logical_not(at_home))
-    def _():
-        greet(lead_row, home)
-
-    for k in range(1, SOLVE_BLOCKS):
-        @pl.when(jnp.logical_and(lead_home, jnp.logical_and(mine >= 1, k > mine)))
+            barrier, inc=1,
+            device_id={"aux": other // n_pair, "pair": lax.rem(other, n_pair)},
+            device_id_type=MESH,
+        )
+        return carry
+
+    lax.fori_loop(1, everyone, greet, 0)
+
+    @pl.when(first)
+    def _():
+        load_inv.wait()
+        inv_hi[own], inv_lo[own] = split(inv[own])
+
+    load_flags.wait()
+    load_dens.wait()
+
+    def flag_of(r, t):
+        return flags[r, t].astype(F32)
+
+    def fit_step(c, total):
+        base = pl.multiple_of(c * STREAM, STREAM)
+        kept = []
+        for r in range(strips):
+            tiles = []
+            for t in range(STREAM // TILE):
+                at = pl.ds(pl.multiple_of(base + t * TILE, TILE), TILE)
+                flag = flag_of(r, c * (STREAM // TILE) + t)
+                tiles.append(dens[:, at] * jnp.full((count, TILE), flag, F32).astype(BF16))
+            kept.append(jnp.concatenate(tiles, 1))
+        load(c).wait()
+        return total + lax.dot_general(
+            jnp.concatenate(kept, 0), masked[:, pl.ds(base, STREAM)], NT, preferred_element_type=F32
+        )
+
+    total = lax.fori_loop(0, chunks, fit_step, jnp.zeros((strips * count, height), F32))
+    for r in range(strips):
+        at = slice(r * TILE, (r + 1) * TILE)
+        fit_out[:, at] = total[r * count:(r + 1) * count, at]
+
+    p_targets = ((1, 0), (2, 0))
+
+    def send_p(c, i):
+        right = pl.ds(c * height, block - c * height)
+        return to_lead(
+            p_out.at[:, right], p_in.at[col, c, :, right], p_send.at[i], p_recv.at[col, c], *p_targets[i]
+        )
+
+    for c in range(members):
+        @pl.when(jnp.logical_and(first, member == c))
         def _():
-            greet(k * members + lead, mine)
-
-    @pl.when(aside)
-    def _():
-        greet(col * members + lead, home_of(col))
-
-    greeted = (
-        n_aux - 1
-        + jnp.where(lead_home, members * (n_pair - 1), 0)
-        + jnp.where(at_home, 0, 1)
-        + jnp.where(jnp.logical_and(lead_home, mine >= 1), SOLVE_BLOCKS - 1 - mine, 0)
-        + jnp.where(aside, 1, 0)
+            right = pl.ds(c * height, block - c * height)
+            p_out[:, right] = dot_split(
+                fit_out[...], inv_hi[own, right], inv_lo[own, right], NN
+            ).astype(p_out.dtype)
+
+    pl.semaphore_wait(barrier, everyone - 1)
+
+    for c in range(members):
+        @pl.when(jnp.logical_and(first, member == c))
+        def _():
+            for i in range(len(p_targets)):
+                send_p(c, i).start()
+
+    send_fit = remote(
+        fit_out, fit_in.at[col, member], fit_send, fit_recv.at[col, member], lead_row, home
     )
-    pl.semaphore_wait(barrier, greeted)
+    sends_fit = jnp.logical_and(later, jnp.logical_not(lead_home))
+
+    @pl.when(sends_fit)
+    def _():
+        send_fit.start()
+
     for c in range(lead):
         @pl.when(member == c)
         def _():
-            @pl.when(at_home)
+            @pl.when(below)
+            def _():
+                move_fac(c).start()
+
+            @pl.when(with_inv)
             def _():
                 move_inv(c).start()
 
-            @pl.when(below)
-            def _():
-                move_fac(c).start()
-
-    load_dens.wait()
-
-    def fit_step(c, total):
-        load(c).wait()
+    def mask_step(c, carry):
         base = pl.multiple_of(c * STREAM, STREAM)
-        for r in range(height // TILE):
+        for r in range(strips):
             for t in range(STREAM // TILE):
-                flag = screen[r, c * (STREAM // TILE) + t].astype(F32)
+                flag = flag_of(r, c * (STREAM // TILE) + t)
                 at = (pl.ds(r * TILE, TILE), pl.ds(pl.multiple_of(base + t * TILE, TILE), TILE))
                 masked[at] = masked[at] * jnp.full((TILE, TILE), flag, F32).astype(BF16)
-        span = pl.ds(base, STREAM)
-        return total + lax.dot_general(
-            dens[:, span], masked[:, span], NT, preferred_element_type=F32
-        )
-
-    fit_out[...] = lax.fori_loop(0, chunks, fit_step, jnp.zeros((dens.shape[0], height), F32))
-
-    send_fit = remote(
-        fit_out, fit_in.at[col, member], fit_send, fit_recv.at[col, member], lead_row, home
-    )
-
-    @pl.when(jnp.logical_not(lead_home))
-    def _():
-        send_fit.start()
-
-    @pl.when(lead_home)
+        return carry
+
+    lax.fori_loop(0, chunks, mask_step, 0)
+
+    @pl.when(lead_below)
+    def _():
+        load_fac.wait()
+        for c in range(lead):
+            move_fac(c).wait_recv()
+        fac_hi[...], fac_lo[...] = split(fac[...])
+
+    @pl.when(lead_inv)
     def _():
         load_inv.wait()
         for c in range(lead):
             move_inv(c).wait_recv()
         inv_hi[...], inv_lo[...] = split(inv[...])
+
+    def prepare_back():
         inv_t_hi[...], inv_t_lo[...] = split(inv[...].T)
-
-    @pl.when(lead_below)
-    def _():
-        load_fac.wait()
+        whole = lax.dot_general(inv_t_hi[...], fac_hi[...], NN, preferred_element_type=F32)
+        whole += lax.dot_general(inv_t_lo[...], fac_hi[...], NN, preferred_element_type=F32)
+        whole += lax.dot_general(inv_t_hi[...], fac_lo[...], NN, preferred_element_type=F32)
+        step_t_hi[...], step_t_lo[...] = split(whole)
+        return whole
+
+    def gather_fit():
+        resid[:, own] = fit_out[...]
         for c in range(lead):
-            move_fac(c).wait_recv()
-
-    @pl.when(lead_aside)
-    def _():
-        fac_hi[...], fac_lo[...] = split(fac[...])
-
-    @pl.when(jnp.logical_and(lead_home, below))
-    def _():
-        high, low = split(fac[...].T)
-        fac_hi[...] = high
-        fac_lo[...] = low
-        whole = lax.dot_general(fac_hi[...], inv_hi[...], NN, preferred_element_type=F32)
-        whole += lax.dot_general(fac_lo[...], inv_hi[...], NN, preferred_element_type=F32)
-        whole += lax.dot_general(fac_hi[...], inv_lo[...], NN, preferred_element_type=F32)
-        step_hi[...], step_lo[...] = split(whole)
-        step_t_hi[...], step_t_lo[...] = split(whole.T)
-
-    recv_s = remote(s_own, s_in, s_send.at[0], s_recv, row, col)
-
-    @pl.when(lead_aside)
-    def _():
-        recv_s.wait_recv()
-        u_out[...] = dot_split(s_in[...], fac_hi[...], fac_lo[...], NT)
-        remote(u_out, u_in.at[col], u_send, u_recv.at[col], row, home).start()
-
-    def send_solved(start):
-        def later(k, carry):
-            copy = remote(s_own, s_in, s_send.at[k], s_recv, k * members + lead, mine)
-            copy.start() if start else copy.wait_send()
-            return carry
-
-        lax.fori_loop(mine + 1, SOLVE_BLOCKS, later, 0)
-
-    def send_rounded(start):
-        for c in range(members):
-            for i in range(n_pair):
-                def one():
-                    copy = remote(
-                        rounded.at[c], rounded.at[c], round_send.at[c, i], round_recv,
-                        mine * members + c, lax.rem(col + i, n_pair),
-                    )
-                    copy.start() if start else copy.wait_send()
-
-                if c != lead or i:
-                    one()
-
-    def send_coef(start):
-        for p in range(n_pair):
-            @pl.when(p < mine - 1)
-            def _():
-                copy = remote(coef, coef, coef_send.at[p], coef_recv, row, p)
-                copy.start() if start else copy.wait_send()
-
-    send_v = remote(
-        v_out, v_in.at[mine], v_send, v_recv.at[mine], col * members + lead, home_of(col)
-    )
-
-    @pl.when(lead_home)
-    def _():
-        resid[:, own] = fit_out[...]
-        for p in range(n_pair):
-            for c in range(members):
-                if c != lead:
-                    @pl.when(p == home)
-                    def _():
-                        remote(fit_out, fit_in.at[p, c], fit_send, fit_recv.at[p, c], row, col).wait_recv()
-                        resid[:, pl.ds(c * height, height)] = fit_in[p, c]
+            for p in range(n_pair):
+                @pl.when(p == home)
+                def _():
+                    remote(fit_out, fit_in.at[p, c], fit_send, fit_recv.at[p, c], row, col).wait_recv()
+                    resid[:, pl.ds(c * height, height)] = fit_in[p, c]
         for p in range(n_pair):
             for c in range(members):
                 @pl.when(p != home)
                 def _():
                     remote(fit_out, fit_in.at[p, c], fit_send, fit_recv.at[p, c], row, col).wait_recv()
                     resid[:, pl.ds(c * height, height)] += fit_in[p, c]
+
+    def gather_start():
         for p in range(n_pair):
-            @pl.when(p < mine - 1)
-            def _():
-                remote(u_out, u_in.at[p], u_send, u_recv.at[p], row, col).wait_recv()
-                resid[...] -= u_in[p]
-        s_own[...] = dot_split(resid[...], inv_hi[...], inv_lo[...], NN)
-
-        @pl.when(below)
+            for c in range(members):
+                right = pl.ds(c * height, block - c * height)
+                remote(
+                    p_out.at[:, right], p_in.at[p, c, :, right], p_send.at[0], p_recv.at[p, c], row, col
+                ).wait_recv()
+        for c in range(members):
+            at = pl.ds(c * height, height)
+            sum_p = p_in[0, 0, :, at].astype(F32)
+            for p in range(n_pair):
+                for d in range(c + 1):
+                    if p or d:
+                        sum_p += p_in[p, d, :, at].astype(F32)
+            start[:, at] = sum_p
+
+    def send_s(i, slot, k, z):
+        return to_lead(s_out.at[slot], s_in, s_send.at[i], s_recv, k, z)
+
+    def send_u(k):
+        return to_lead(u_out, u_in.at[col], u_send, u_recv.at[col], k, k - 1)
+
+    def send_v(k, z):
+        return to_lead(v_out, v_in.at[mine, col], v_send, v_recv.at[mine, col], k, z)
+
+    def send_w(i, slot, k, z):
+        return to_lead(w_out.at[slot], w_in, w_send.at[i], w_recv, k, z)
+
+    def wait_s():
+        send_s(0, 0, 0, 0).wait_recv()
+
+    def take_u(p):
+        remote(u_out, u_in.at[p], u_send, u_recv.at[p], row, col).wait_recv()
+        resid[...] -= u_in[p].astype(F32)
+
+    def take_v(k, z):
+        remote(v_out, v_in.at[k, z], v_send, v_recv.at[k, z], row, col).wait_recv()
+        return v_in[k, z].astype(F32)
+
+    def wait_w():
+        send_w(0, 0, 0, 0).wait_recv()
+
+    def round_copy(k, c, i, z):
+        return remote(
+            rounded.at[c], rounded.at[c], round_send.at[c, i], round_recv, k * members + c, lax.rem(z + i, n_pair)
+        )
+
+    def spread_rounded(k, go):
+        for i in reversed(range(n_pair)):
+            for c in range(members):
+                if c != lead or i:
+                    copy = round_copy(k, c, i, k - 1)
+                    copy.start() if go else copy.wait_send()
+
+    def finish(k, values):
+        coef = dot_split(values, inv_t_hi[...], inv_t_lo[...], NN)
+        for c in range(members):
+            rounded[c] = coef[:, c * height:(c + 1) * height].astype(BF16)
+        spread_rounded(k, True)
+
+    def last_copy(c, z):
+        right = pl.ds(c * height, block - c * height)
+        return remote(
+            last_out.at[:, right], last_in.at[:, right], last_send.at[c, z], last_recv, c, z
+        )
+
+    @pl.when(role(1, 0))
+    def _():
+        gather_fit()
+        gather_start()
+        s_out[0] = start[...].astype(s_out.dtype)
+        send_s(2, 0, 3, 0).start()
+        resid[...] -= dot_split(start[...], fac_hi[...], fac_lo[...], NT)
+        solved[...] = dot_split(resid[...], inv_hi[...], inv_lo[...], NN)
+        s_out[1] = solved[...].astype(s_out.dtype)
+        send_s(0, 1, 2, 1).start()
+        send_s(1, 1, 3, 1).start()
+        prepare_back()
+        solved[...] -= take_v(3, 1)
+        start[...] -= take_v(3, 0)
+        solved[...] -= take_v(2, 1)
+        back = apply(solved[...].astype(w_out.dtype), step_t_hi[...], step_t_lo[...], NN)
+        last_out[...] = (start[...] - take_v(2, 0) - back).astype(last_out.dtype)
+        for z in reversed(range(n_pair)):
+            for c in range(members):
+                last_copy(c, z).start()
+        finish(1, solved[...])
+
+    @pl.when(role(2, 0))
+    def _():
+        gather_start()
+        u_out[...] = dot_split(start[...], fac_hi[...], fac_lo[...], NT).astype(u_out.dtype)
+        send_u(2).start()
+        prepare_back()
+        wait_w()
+        v_out[...] = apply(w_in[...], step_t_hi[...], step_t_lo[...], NN).astype(v_out.dtype)
+        send_v(1, 0).start()
+
+    @pl.when(jnp.logical_or(role(3, 0), role(3, 1)))
+    def _():
+        wait_s()
+        u_out[...] = apply(s_in[...], fac_hi[...], fac_lo[...], NT).astype(u_out.dtype)
+        send_u(3).start()
+        wait_w()
+        v_out[...] = apply(w_in[...], fac_hi[...], fac_lo[...], NN).astype(v_out.dtype)
+        send_v(1, 0).start()
+
+    @pl.when(role(2, 1))
+    def _():
+        gather_fit()
+        take_u(0)
+        wait_s()
+        resid[...] -= apply(s_in[...], fac_hi[...], fac_lo[...], NT)
+        solved[...] = dot_split(resid[...], inv_hi[...], inv_lo[...], NN)
+        s_out[0] = solved[...].astype(s_out.dtype)
+        send_s(0, 0, 3, 2).start()
+        prepare_back()
+        solved[...] -= take_v(3, 2)
+        v_out[...] = apply(
+            solved[...].astype(w_out.dtype), step_t_hi[...], step_t_lo[...], NN
+        ).astype(v_out.dtype)
+        send_v(1, 0).start()
+        finish(2, solved[...])
+
+    @pl.when(role(3, 2))
+    def _():
+        whole = prepare_back()
+        step_hi[...], step_lo[...] = split(whole.T)
+        gather_fit()
+        take_u(0)
+        take_u(1)
+        resid[...] = dot_split(resid[...], inv_hi[...], inv_lo[...], NN)
+        wait_s()
+        solved[...] = resid[...] - apply(s_in[...], step_hi[...], step_lo[...], NN)
+        back = apply(solved[...].astype(w_out.dtype), step_t_hi[...], step_t_lo[...], NN)
+        v_out[...] = back.astype(v_out.dtype)
+        send_v(2, 1).start()
+        w_out[1] = (s_in[...].astype(F32) - back).astype(w_out.dtype)
+        send_w(2, 1, 2, 0).start()
+        coef = dot_split(solved[...], inv_t_hi[...], inv_t_lo[...], NN)
+        w_out[0] = coef.astype(w_out.dtype)
+        send_w(0, 0, 3, 0).start()
+        send_w(1, 0, 3, 1).start()
+        for c in range(members):
+            rounded[c] = coef[:, c * height:(c + 1) * height].astype(BF16)
+        spread_rounded(3, True)
+
+    @pl.when(jnp.logical_and(later, jnp.logical_not(lead_home)))
+    def _():
+        remote(rounded.at[0], rounded.at[0], round_send.at[0, 0], round_recv, row, col).wait_recv()
+
+    for c in range(members):
+        @pl.when(jnp.logical_and(first, member == c))
         def _():
-            recv_s.wait_recv()
-            s_own[...] -= dot_split(s_in[...], step_hi[...], step_lo[...], NN)
-
-        send_solved(True)
-
-        resid[...] = s_own[...]
-
-        def subtract(i, carry):
-            source = SOLVE_BLOCKS - 1 - i
-            remote(v_out, v_in.at[source], v_send, v_recv.at[source], row, col).wait_recv()
-            resid[...] -= v_in[source]
-            return carry
-
-        lax.fori_loop(0, SOLVE_BLOCKS - 1 - mine, subtract, 0)
-
-        @pl.when(below)
-        def _():
-            v_out[...] = dot_split(resid[...], step_t_hi[...], step_t_lo[...], NN)
-            send_v.start()
-
-        coef[...] = dot_split(resid[...], inv_t_hi[...], inv_t_lo[...], NN)
-        for c in range(members):
-            rounded[c] = coef[:, pl.ds(c * height, height)].astype(BF16)
-        send_coef(True)
-        send_rounded(True)
-
-    @pl.when(lead_aside)
-    def _():
-        remote(coef, coef, coef_send.at[0], coef_recv, row, col).wait_recv()
-        v_out[...] = dot_split(coef[...], fac_hi[...], fac_lo[...], NN)
-        send_v.start()
-
-    @pl.when(jnp.logical_not(lead_home))
-    def _():
-        remote(rounded.at[0], rounded.at[0], round_send.at[0, 0], round_recv, row, col).wait_recv()
+            right = pl.ds(c * height, block - c * height)
+            remote(
+                last_out.at[:, right], last_in.at[:, right], last_send.at[c, 0], last_recv, row, col
+            ).wait_recv()
+            rounded[c] = apply(last_in[:, right], inv_hi[own, right], inv_lo[own, right], NT).astype(BF16)
 
     mine_rounded = rounded[member]
 
@@ -629,31 +752,57 @@
     for c in range(lead):
         @pl.when(member == c)
         def _():
-            @pl.when(at_home)
+            @pl.when(below)
+            def _():
+                move_fac(c).wait_send()
+
+            @pl.when(with_inv)
             def _():
                 move_inv(c).wait_send()
 
-            @pl.when(below)
-            def _():
-                move_fac(c).wait_send()
-
-    @pl.when(jnp.logical_not(lead_home))
+    for c in range(members):
+        @pl.when(jnp.logical_and(first, member == c))
+        def _():
+            for i in range(len(p_targets)):
+                send_p(c, i).wait_send()
+
+    @pl.when(sends_fit)
     def _():
         send_fit.wait_send()
 
-    @pl.when(lead_aside)
-    def _():
-        remote(u_out, u_in.at[col], u_send, u_recv.at[col], row, home).wait_send()
-
-    @pl.when(lead_below)
-    def _():
-        send_v.wait_send()
-
-    @pl.when(lead_home)
-    def _():
-        send_solved(False)
-        send_coef(False)
-        send_rounded(False)
+    @pl.when(role(1, 0))
+    def _():
+        send_s(2, 0, 3, 0).wait_send()
+        send_s(0, 1, 2, 1).wait_send()
+        send_s(1, 1, 3, 1).wait_send()
+        for z in range(n_pair):
+            for c in range(members):
+                last_copy(c, z).wait_send()
+        spread_rounded(1, False)
+
+    @pl.when(role(2, 0))
+    def _():
+        send_u(2).wait_send()
+        send_v(1, 0).wait_send()
+
+    @pl.when(jnp.logical_or(role(3, 0), role(3, 1)))
+    def _():
+        send_u(3).wait_send()
+        send_v(1, 0).wait_send()
+
+    @pl.when(role(2, 1))
+    def _():
+        send_s(0, 0, 3, 2).wait_send()
+        send_v(1, 0).wait_send()
+        spread_rounded(2, False)
+
+    @pl.when(role(3, 2))
+    def _():
+        send_v(2, 1).wait_send()
+        send_w(2, 1, 2, 0).wait_send()
+        send_w(0, 0, 3, 0).wait_send()
+        send_w(1, 0, 3, 1).wait_send()
+        spread_rounded(3, False)
 
     def sent(i, carry):
         part_copy(i)[1].wait_send()
@@ -674,27 +823,34 @@
     def rows(*lead):
         return vmem(lead + (count, height), F32)
 
-    def whole(*lead):
-        return vmem(lead + (count, block), F32)
+    def whole(*lead, kind=F32):
+        return vmem(lead + (count, block), kind)
 
     weights = 2 * block * block * 4 + 10 * block * block * 2
-    if breadth == block and weights + integrals.size * 2 <= VMEM_ROOM:
+    fits = weights + integrals.size * 2 <= VMEM_ROOM
+    if breadth == block and members == 2 and n_pair == SOLVE_BLOCKS and fits:
         body = lead_kernel
+        screen_space = pl.ANY
         scratch = [
-            vmem((height, width), BF16), vmem((count, width), BF16),
+            pltpu.SMEM(screen.shape, screen.dtype), vmem((height, width), BF16), vmem((count, width), BF16),
             vmem((block, block), F32), vmem((block, block), F32),
             *[vmem((block, block), BF16) for _ in range(10)],
-            rows(), rows(n_pair, members), whole(), whole(n_pair), whole(), whole(), whole(), whole(),
-            vmem((members, count, height), BF16), whole(), whole(SOLVE_BLOCKS),
+            rows(), rows(n_pair, members), whole(kind=P_KIND), whole(n_pair, members, kind=P_KIND),
+            whole(kind=U_KIND), whole(n_pair, kind=U_KIND), whole(2, kind=S_KIND), whole(kind=S_KIND),
+            whole(2, kind=BF16), whole(kind=BF16), whole(kind=V_KIND), whole(SOLVE_BLOCKS, n_pair, kind=V_KIND),
+            whole(), whole(), whole(), vmem((members, count, height), BF16),
+            whole(kind=L_KIND), whole(kind=L_KIND),
             vmem((n_aux, count, share), BF16), vmem((n_aux, count, share), BF16),
-            dma((width // STREAM,)), dma((3,)),
+            dma((width // STREAM,)), dma((4,)),
             dma, dma((members,)), dma, dma((members,)),
-            dma, dma((n_pair, members)), dma, dma((n_pair,)), dma((SOLVE_BLOCKS,)), dma,
-            dma((n_pair,)), dma, dma((members, n_pair)), dma, dma, dma((SOLVE_BLOCKS,)),
+            dma, dma((n_pair, members)), dma((2,)), dma((n_pair, members)), dma, dma((n_pair,)),
+            dma((3,)), dma, dma((3,)), dma, dma, dma((SOLVE_BLOCKS, n_pair)),
+            dma((members, n_pair)), dma, dma((members, n_pair)), dma,
             dma((n_aux,)), dma((n_aux,)),
         ]
     else:
         body = spread_kernel
+        screen_space = pltpu.SMEM
         scratch = [
             vmem((height, width), BF16), vmem((count, width), BF16),
             vmem((height, breadth), F32), vmem((height, block), F32),
@@ -717,7 +873,7 @@
         in_specs=[
             pl.BlockSpec(memory_space=pl.ANY),
             pl.BlockSpec(memory_space=pl.ANY),
-            pl.BlockSpec(memory_space=pltpu.SMEM),
+            pl.BlockSpec(memory_space=screen_space),
             pl.BlockSpec(memory_space=pl.ANY),
             pl.BlockSpec(memory_space=pl.ANY),
         ],

time: 43.7 us -> 40.6 us (0.929)
  the two profiles are of different devices: /device:TPU:10 before, /device:TPU:12 now
where the time goes in v1:
time: 40.6 us; the launch traced here: 40.4 us
  Pallas kernels  38.9 us (96%)
  local copies, waits for them, and re-layouts  1.47 us (4%)
    pallas_call x1, Pallas kernels, shards(): pl.pallas_call(functools.partial(body, n_aux, n_pair), out_shape=jax.Shap...  38.9 us
    unnamed x1, local copies, waits for them, and re-layouts  1.47 us

profile of v1, /device:TPU:12, one launch (start us, length us, event | category | flops | bytes accessed | tf_op | source)
XLA Modules:
  0.0 40.4 jit_solution(5937333308645866421)
XLA Ops:
  0.0 38.9 %shard_map.55 = f32[16,1024]{1,0:T(8,128)} custom-call(bf16[384,8192]{1,0:T(8,128)(2,1)} %integrals.1, bf16[16,8192]{1,0:T(8,128)(2,1)} %densities.1, s32[3,64]{1,0:T(4,128)} %screen.1, f32[384,768]{1,0:T(8,128)} %factor.1, f32[384,768]{1,0:T(8,128)} %diag_inv.1), custom_call_target="tpu_custom_call" | custom-call | tf_op jit(solution)/shard_map/pallas_call | solution.py:870
  38.9 1.5 %copy.7 = f32[16,1024]{1,0:T(8,128)} copy(f32[16,1024]{1,0:T(8,128)} %shard_map.55) | data formatting | bytes 131072

commit v2 on v1

--- a/solution.py
+++ b/solution.py
@@ -10,13 +10,15 @@
 TILE = 128
 SOLVE_BLOCKS = 4
 STREAM = 1024
+LEAD_STREAM = 2048
 VMEM_ROOM = 48 * 2**20
 MESH = pl.DeviceIdType.MESH
 NN = (((1,), (0,)), ((), ()))
 NT = (((1,), (1,)), ((), ()))
 F32 = jnp.float32
 BF16 = jnp.bfloat16
-P_KIND, S_KIND, U_KIND, V_KIND, L_KIND = BF16, BF16, F32, BF16, BF16
+P_KIND, S_KIND, V_KIND, L_KIND = BF16, BF16, BF16, BF16
+VMEM_LIMIT = 56400000
 
 
 def split(values):
@@ -336,18 +338,18 @@
     integrals, densities, screen, factor, diag_inv, out,
     flags, masked, dens, fac, inv, fac_hi, fac_lo, inv_hi, inv_lo, inv_t_hi, inv_t_lo,
     step_hi, step_lo, step_t_hi, step_t_lo,
-    fit_out, fit_in, p_out, p_in, u_out, u_in, s_out, s_in, w_out, w_in, v_out, v_in,
+    fit_out, fit_in, p_out, p_in, u_out, u_in, s_out, s_in, t_out, t_in, w_out, w_in, v_out, v_in, y_out, y_in,
     resid, solved, start, rounded, last_out, last_in, part_out, part_in,
     load_sem, small_sem, fac_send, fac_recv, inv_send, inv_recv,
-    fit_send, fit_recv, p_send, p_recv, u_send, u_recv, s_send, s_recv, w_send, w_recv,
-    v_send, v_recv, round_send, round_recv, last_send, last_recv, part_send, part_recv,
+    fit_send, fit_recv, p_send, p_recv, u_send, u_recv, s_send, s_recv, t_send, t_recv, w_send, w_recv,
+    v_send, v_recv, y_send, y_recv, round_send, round_recv, last_send, last_recv, part_send, part_recv,
 ):
     height, width = masked.shape
     block = inv.shape[1]
     count = dens.shape[0]
     members = block // height
     share = width // n_aux
-    chunks = width // STREAM
+    chunks = width // LEAD_STREAM
     strips = height // TILE
 
     row = lax.axis_index("aux")
@@ -371,7 +373,6 @@
 
     lead_home = jnp.logical_and(is_lead, at_home)
     lead_below = jnp.logical_and(is_lead, below)
-    with_inv = jnp.logical_or(at_home, chip(2, 0))
 
     def remote(src, dst, send, recv, aux, pair):
         return pltpu.make_async_remote_copy(
@@ -383,7 +384,7 @@
         return remote(src, dst, send, recv, k * members + lead, z)
 
     def load(c):
-        at = pl.ds(pl.multiple_of(c * STREAM, STREAM), STREAM)
+        at = pl.ds(pl.multiple_of(c * LEAD_STREAM, LEAD_STREAM), LEAD_STREAM)
         return pltpu.make_async_copy(integrals.at[:, at], masked.at[:, at], load_sem.at[c])
 
     own = pl.ds(lead * height, height)
@@ -402,46 +403,79 @@
             inv_send, inv_recv.at[c], lead_row, col,
         )
 
-    lead_inv = jnp.logical_and(is_lead, with_inv)
+    def load_start(c):
+        right = pl.ds(c * height, block - c * height)
+        return pltpu.make_async_copy(diag_inv.at[:, right], inv.at[own, right], small_sem.at[2])
+
     load_flags.start()
     load_dens.start()
-
-    @pl.when(first)
-    def _():
-        load_inv.start()
-
     for c in range(chunks):
         load(c).start()
-
-    @pl.when(lead_inv)
-    def _():
+    for c in range(members):
+        @pl.when(jnp.logical_and(first, member == c))
+        def _():
+            load_start(c).start()
+
+
+    @pl.when(lead_below)
+    def _():
+        load_fac.start()
         load_inv.start()
-        for c in range(1, lead):
-            inv[pl.ds(c * height, height), pl.ds(0, c * height)] = jnp.zeros((height, c * height), F32)
-
-    @pl.when(lead_below)
-    def _():
-        load_fac.start()
 
     barrier = pltpu.get_barrier_semaphore()
-    everyone = n_aux * n_pair
-    me = row * n_pair + col
-
-    def greet(i, carry):
-        other = lax.rem(me + i, everyone)
+
+    def greet(k, c, z):
         pl.semaphore_signal(
-            barrier, inc=1,
-            device_id={"aux": other // n_pair, "pair": lax.rem(other, n_pair)},
-            device_id_type=MESH,
-        )
-        return carry
-
-    lax.fori_loop(1, everyone, greet, 0)
-
-    @pl.when(first)
-    def _():
-        load_inv.wait()
-        inv_hi[own], inv_lo[own] = split(inv[own])
+            barrier, inc=1, device_id={"aux": k * members + c, "pair": z}, device_id_type=MESH
+        )
+
+    c_one, c_two, c_three = role(1, 0), role(2, 1), role(3, 2)
+    lead_aside = jnp.logical_and(lead_below, jnp.logical_not(at_home))
+
+    @pl.when(jnp.logical_or(c_one, role(2, 0)))
+    def _():
+        for c in range(members):
+            for z in range(n_pair):
+                greet(0, c, z)
+
+    @pl.when(lead_home)
+    def _():
+        for c in range(members):
+            for i in range(n_pair):
+                if c != lead or i:
+                    greet(mine, c, lax.rem(col + i, n_pair))
+
+    @pl.when(lead_aside)
+    def _():
+        for c in range(lead):
+            greet(mine, c, col)
+
+    @pl.when(jnp.logical_or(c_two, jnp.logical_and(lead_aside, mine == 3)))
+    def _():
+        greet(1, lead, 0)
+
+    @pl.when(c_three)
+    def _():
+        greet(2, lead, 1)
+
+    gives = jnp.logical_and(jnp.logical_not(is_lead), below)
+    greeted = (
+        jnp.where(first, 2, 0)
+        + jnp.where(jnp.logical_and(later, jnp.logical_not(lead_home)), 1, 0)
+        + jnp.where(jnp.logical_and(gives, jnp.logical_not(at_home)), 1, 0)
+        + jnp.where(c_one, 3, 0)
+        + jnp.where(c_two, 1, 0)
+    )
+
+    @pl.when(gives)
+    def _():
+        pl.semaphore_wait(barrier, greeted)
+
+    for c in range(lead):
+        @pl.when(jnp.logical_and(gives, member == c))
+        def _():
+            move_fac(c).start()
+            move_inv(c).start()
 
     load_flags.wait()
     load_dens.wait()
@@ -449,25 +483,38 @@
     def flag_of(r, t):
         return flags[r, t].astype(F32)
 
-    def fit_step(c, total):
-        base = pl.multiple_of(c * STREAM, STREAM)
+    def fit_step(c, sums):
+        base = pl.multiple_of(c * LEAD_STREAM, LEAD_STREAM)
         kept = []
         for r in range(strips):
             tiles = []
-            for t in range(STREAM // TILE):
+            for t in range(LEAD_STREAM // TILE):
                 at = pl.ds(pl.multiple_of(base + t * TILE, TILE), TILE)
-                flag = flag_of(r, c * (STREAM // TILE) + t)
+                flag = flag_of(r, c * (LEAD_STREAM // TILE) + t)
                 tiles.append(dens[:, at] * jnp.full((count, TILE), flag, F32).astype(BF16))
             kept.append(jnp.concatenate(tiles, 1))
         load(c).wait()
-        return total + lax.dot_general(
-            jnp.concatenate(kept, 0), masked[:, pl.ds(base, STREAM)], NT, preferred_element_type=F32
-        )
-
-    total = lax.fori_loop(0, chunks, fit_step, jnp.zeros((strips * count, height), F32))
+        return tuple(
+            sums[r] + lax.dot_general(
+                kept[r], masked[pl.ds(r * TILE, TILE), pl.ds(base, LEAD_STREAM)], NT,
+                preferred_element_type=F32,
+            )
+            for r in range(strips)
+        )
+
+    sums = lax.fori_loop(
+        0, chunks - 1, fit_step, tuple(jnp.zeros((count, TILE), F32) for _ in range(strips))
+    )
+    for c in range(members):
+        @pl.when(jnp.logical_and(first, member == c))
+        def _():
+            right = pl.ds(c * height, block - c * height)
+            load_start(c).wait()
+            inv_hi[own, right], inv_lo[own, right] = split(inv[own, right])
+
+    sums = fit_step(chunks - 1, sums)
     for r in range(strips):
-        at = slice(r * TILE, (r + 1) * TILE)
-        fit_out[:, at] = total[r * count:(r + 1) * count, at]
+        fit_out[:, pl.ds(r * TILE, TILE)] = sums[r]
 
     p_targets = ((1, 0), (2, 0))
 
@@ -485,7 +532,10 @@
                 fit_out[...], inv_hi[own, right], inv_lo[own, right], NN
             ).astype(p_out.dtype)
 
-    pl.semaphore_wait(barrier, everyone - 1)
+    @pl.when(jnp.logical_not(jnp.logical_or(gives, c_three)))
+    def _():
+        pl.semaphore_wait(barrier, greeted)
+
 
     for c in range(members):
         @pl.when(jnp.logical_and(first, member == c))
@@ -502,22 +552,11 @@
     def _():
         send_fit.start()
 
-    for c in range(lead):
-        @pl.when(member == c)
-        def _():
-            @pl.when(below)
-            def _():
-                move_fac(c).start()
-
-            @pl.when(with_inv)
-            def _():
-                move_inv(c).start()
-
     def mask_step(c, carry):
-        base = pl.multiple_of(c * STREAM, STREAM)
+        base = pl.multiple_of(c * LEAD_STREAM, LEAD_STREAM)
         for r in range(strips):
-            for t in range(STREAM // TILE):
-                flag = flag_of(r, c * (STREAM // TILE) + t)
+            for t in range(LEAD_STREAM // TILE):
+                flag = flag_of(r, c * (LEAD_STREAM // TILE) + t)
                 at = (pl.ds(r * TILE, TILE), pl.ds(pl.multiple_of(base + t * TILE, TILE), TILE))
                 masked[at] = masked[at] * jnp.full((TILE, TILE), flag, F32).astype(BF16)
         return carry
@@ -530,9 +569,6 @@
         for c in range(lead):
             move_fac(c).wait_recv()
         fac_hi[...], fac_lo[...] = split(fac[...])
-
-    @pl.when(lead_inv)
-    def _():
         load_inv.wait()
         for c in range(lead):
             move_inv(c).wait_recv()
@@ -545,6 +581,13 @@
         whole += lax.dot_general(inv_t_hi[...], fac_lo[...], NN, preferred_element_type=F32)
         step_t_hi[...], step_t_lo[...] = split(whole)
         return whole
+
+    def prepare_ahead():
+        whole = prepare_back()
+        step_hi[...], step_lo[...] = split(whole.T)
+
+    def turn_fac():
+        step_hi[...], step_lo[...] = split(fac[...].T)
 
     def gather_fit():
         resid[:, own] = fit_out[...]
@@ -577,28 +620,38 @@
                         sum_p += p_in[p, d, :, at].astype(F32)
             start[:, at] = sum_p
 
-    def send_s(i, slot, k, z):
-        return to_lead(s_out.at[slot], s_in, s_send.at[i], s_recv, k, z)
+    def send_s(k, z):
+        return to_lead(s_out, s_in, s_send, s_recv, k, z)
+
+    def send_t(slot, k, z):
+        return to_lead(t_out.at[slot], t_in, t_send.at[slot], t_recv, k, z)
 
     def send_u(k):
         return to_lead(u_out, u_in.at[col], u_send, u_recv.at[col], k, k - 1)
 
     def send_v(k, z):
-        return to_lead(v_out, v_in.at[mine, col], v_send, v_recv.at[mine, col], k, z)
+        return to_lead(v_out, v_in, v_send, v_recv, k, z)
+
+    def send_y():
+        return to_lead(y_out, y_in.at[mine, col], y_send, y_recv.at[mine, col], 1, 0)
 
     def send_w(i, slot, k, z):
         return to_lead(w_out.at[slot], w_in, w_send.at[i], w_recv, k, z)
 
     def wait_s():
-        send_s(0, 0, 0, 0).wait_recv()
+        send_s(0, 0).wait_recv()
 
     def take_u(p):
         remote(u_out, u_in.at[p], u_send, u_recv.at[p], row, col).wait_recv()
         resid[...] -= u_in[p].astype(F32)
 
-    def take_v(k, z):
-        remote(v_out, v_in.at[k, z], v_send, v_recv.at[k, z], row, col).wait_recv()
-        return v_in[k, z].astype(F32)
+    def take_v():
+        remote(v_out, v_in, v_send, v_recv, row, col).wait_recv()
+        return v_in[...].astype(F32)
+
+    def take_y(k, z):
+        remote(y_out, y_in.at[k, z], y_send, y_recv.at[k, z], row, col).wait_recv()
+        return y_in[k, z]
 
     def wait_w():
         send_w(0, 0, 0, 0).wait_recv()
@@ -629,21 +682,23 @@
 
     @pl.when(role(1, 0))
     def _():
+        turn_fac()
         gather_fit()
         gather_start()
-        s_out[0] = start[...].astype(s_out.dtype)
-        send_s(2, 0, 3, 0).start()
-        resid[...] -= dot_split(start[...], fac_hi[...], fac_lo[...], NT)
+        t_out[0] = start[...]
+        send_t(0, 3, 0).start()
+        resid[...] -= dot_split(start[...], step_hi[...], step_lo[...], NN)
         solved[...] = dot_split(resid[...], inv_hi[...], inv_lo[...], NN)
-        s_out[1] = solved[...].astype(s_out.dtype)
-        send_s(0, 1, 2, 1).start()
-        send_s(1, 1, 3, 1).start()
+        s_out[...] = solved[...].astype(s_out.dtype)
+        t_out[1] = solved[...]
+        send_s(2, 1).start()
+        send_t(1, 3, 1).start()
         prepare_back()
-        solved[...] -= take_v(3, 1)
-        start[...] -= take_v(3, 0)
-        solved[...] -= take_v(2, 1)
-        back = apply(solved[...].astype(w_out.dtype), step_t_hi[...], step_t_lo[...], NN)
-        last_out[...] = (start[...] - take_v(2, 0) - back).astype(last_out.dtype)
+        solved[...] -= take_y(3, 1)
+        start[...] -= take_y(3, 0)
+        solved[...] -= take_v()
+        back = dot_split(solved[...], step_t_hi[...], step_t_lo[...], NN)
+        last_out[...] = (start[...] - take_y(2, 0) - back).astype(last_out.dtype)
         for z in reversed(range(n_pair)):
             for c in range(members):
                 last_copy(c, z).start()
@@ -651,59 +706,58 @@
 
     @pl.when(role(2, 0))
     def _():
+        turn_fac()
         gather_start()
-        u_out[...] = dot_split(start[...], fac_hi[...], fac_lo[...], NT).astype(u_out.dtype)
+        u_out[...] = dot_split(start[...], step_hi[...], step_lo[...], NN)
         send_u(2).start()
         prepare_back()
         wait_w()
-        v_out[...] = apply(w_in[...], step_t_hi[...], step_t_lo[...], NN).astype(v_out.dtype)
-        send_v(1, 0).start()
+        y_out[...] = dot_split(w_in[...], step_t_hi[...], step_t_lo[...], NN)
+        send_y().start()
 
     @pl.when(jnp.logical_or(role(3, 0), role(3, 1)))
     def _():
-        wait_s()
-        u_out[...] = apply(s_in[...], fac_hi[...], fac_lo[...], NT).astype(u_out.dtype)
+        prepare_ahead()
+        send_t(0, 0, 0).wait_recv()
+        u_out[...] = dot_split(t_in[...], step_hi[...], step_lo[...], NN)
         send_u(3).start()
         wait_w()
-        v_out[...] = apply(w_in[...], fac_hi[...], fac_lo[...], NN).astype(v_out.dtype)
-        send_v(1, 0).start()
+        y_out[...] = dot_split(w_in[...], step_t_hi[...], step_t_lo[...], NN)
+        send_y().start()
 
     @pl.when(role(2, 1))
     def _():
+        prepare_ahead()
         gather_fit()
         take_u(0)
-        wait_s()
-        resid[...] -= apply(s_in[...], fac_hi[...], fac_lo[...], NT)
-        solved[...] = dot_split(resid[...], inv_hi[...], inv_lo[...], NN)
-        s_out[0] = solved[...].astype(s_out.dtype)
-        send_s(0, 0, 3, 2).start()
-        prepare_back()
-        solved[...] -= take_v(3, 2)
-        v_out[...] = apply(
-            solved[...].astype(w_out.dtype), step_t_hi[...], step_t_lo[...], NN
-        ).astype(v_out.dtype)
-        send_v(1, 0).start()
-        finish(2, solved[...])
-
-    @pl.when(role(3, 2))
-    def _():
-        whole = prepare_back()
-        step_hi[...], step_lo[...] = split(whole.T)
-        gather_fit()
-        take_u(0)
-        take_u(1)
         resid[...] = dot_split(resid[...], inv_hi[...], inv_lo[...], NN)
         wait_s()
         solved[...] = resid[...] - apply(s_in[...], step_hi[...], step_lo[...], NN)
-        back = apply(solved[...].astype(w_out.dtype), step_t_hi[...], step_t_lo[...], NN)
+        s_out[...] = solved[...].astype(s_out.dtype)
+        send_s(3, 2).start()
+        solved[...] -= take_v()
+        v_out[...] = dot_split(solved[...], step_t_hi[...], step_t_lo[...], NN).astype(v_out.dtype)
+        send_v(1, 0).start()
+        finish(2, solved[...])
+
+    @pl.when(role(3, 2))
+    def _():
+        prepare_ahead()
+        gather_fit()
+        resid[...] = dot_split(resid[...], inv_hi[...], inv_lo[...], NN)
+        take_u(0)
+        take_u(1)
+        wait_s()
+        solved[...] = resid[...] - apply(s_in[...], step_hi[...], step_lo[...], NN)
+        w_out[0] = solved[...]
+        send_w(0, 0, 3, 1).start()
+        send_w(1, 0, 3, 0).start()
+        back = dot_split(solved[...], step_t_hi[...], step_t_lo[...], NN)
         v_out[...] = back.astype(v_out.dtype)
         send_v(2, 1).start()
-        w_out[1] = (s_in[...].astype(F32) - back).astype(w_out.dtype)
+        w_out[1] = s_in[...].astype(F32) - back
         send_w(2, 1, 2, 0).start()
         coef = dot_split(solved[...], inv_t_hi[...], inv_t_lo[...], NN)
-        w_out[0] = coef.astype(w_out.dtype)
-        send_w(0, 0, 3, 0).start()
-        send_w(1, 0, 3, 1).start()
         for c in range(members):
             rounded[c] = coef[:, c * height:(c + 1) * height].astype(BF16)
         spread_rounded(3, True)
@@ -723,31 +777,51 @@
 
     mine_rounded = rounded[member]
 
-    def product(target):
-        span = pl.ds(pl.multiple_of(target * share, TILE), share)
-        return lax.dot_general(mine_rounded, masked[:, span], NN, preferred_element_type=F32)
-
-    def part_copy(i):
-        target = lax.rem(row + n_aux - i, n_aux)
-        return target, remote(
+    span = members * share
+
+    def product(group):
+        at = pl.ds(pl.multiple_of(group * span, TILE), span)
+        return lax.dot_general(mine_rounded, masked[:, at], NN, preferred_element_type=F32)
+
+    def flipped(mask):
+        group, unit = 0, 1
+        while unit * members < n_aux:
+            digit = lax.rem(mine // unit, 2)
+            group = group + unit * (1 - digit if mask & unit else digit)
+            unit *= 2
+        return group
+
+    order = sorted(range(1, n_aux // members), key=lambda m: -bin(m).count("1"))
+    partner = mine * members + 1 - member
+
+    def part_copy(target):
+        return remote(
             part_out.at[target], part_in.at[row], part_send.at[target], part_recv.at[row], target, col
         )
 
-    def give(i, carry):
-        target, copy = part_copy(i)
-        part_out[target] = product(target).astype(BF16)
-        copy.start()
-        return carry
-
-    lax.fori_loop(1, n_aux, give, 0)
-    total = product(row)
-
-    def take(i, total):
-        source = lax.rem(row + i, n_aux)
+    for mask in order:
+        group = flipped(mask)
+        values = product(group)
+        for c in range(members):
+            part_out[group * members + c] = values[:, c * share:(c + 1) * share].astype(BF16)
+            part_copy(group * members + c).start()
+
+    values = product(mine)
+    halves = values[:, :share], values[:, share:]
+    part_out[partner] = jnp.where(member == 0, halves[1], halves[0]).astype(BF16)
+    part_copy(partner).start()
+    total = jnp.where(member == 0, halves[0], halves[1])
+
+    def take(source):
         remote(part_out.at[0], part_in.at[source], part_send.at[0], part_recv.at[source], row, col).wait_recv()
-        return total + part_in[source].astype(F32)
-
-    out[...] = lax.fori_loop(1, n_aux, take, total)
+        return part_in[source].astype(F32)
+
+    total += take(partner)
+    for mask in reversed(order):
+        for c in range(members):
+            total += take(flipped(mask) * members + c)
+
+    out[...] = total
 
     for c in range(lead):
         @pl.when(member == c)
@@ -755,9 +829,6 @@
             @pl.when(below)
             def _():
                 move_fac(c).wait_send()
-
-            @pl.when(with_inv)
-            def _():
                 move_inv(c).wait_send()
 
     for c in range(members):
@@ -772,9 +843,9 @@
 
     @pl.when(role(1, 0))
     def _():
-        send_s(2, 0, 3, 0).wait_send()
-        send_s(0, 1, 2, 1).wait_send()
-        send_s(1, 1, 3, 1).wait_send()
+        send_t(0, 3, 0).wait_send()
+        send_s(2, 1).wait_send()
+        send_t(1, 3, 1).wait_send()
         for z in range(n_pair):
             for c in range(members):
                 last_copy(c, z).wait_send()
@@ -783,16 +854,16 @@
     @pl.when(role(2, 0))
     def _():
         send_u(2).wait_send()
-        send_v(1, 0).wait_send()
+        send_y().wait_send()
 
     @pl.when(jnp.logical_or(role(3, 0), role(3, 1)))
     def _():
         send_u(3).wait_send()
-        send_v(1, 0).wait_send()
+        send_y().wait_send()
 
     @pl.when(role(2, 1))
     def _():
-        send_s(0, 0, 3, 2).wait_send()
+        send_s(3, 2).wait_send()
         send_v(1, 0).wait_send()
         spread_rounded(2, False)
 
@@ -800,15 +871,14 @@
     def _():
         send_v(2, 1).wait_send()
         send_w(2, 1, 2, 0).wait_send()
-        send_w(0, 0, 3, 0).wait_send()
-        send_w(1, 0, 3, 1).wait_send()
+        send_w(0, 0, 3, 1).wait_send()
+        send_w(1, 0, 3, 0).wait_send()
         spread_rounded(3, False)
 
-    def sent(i, carry):
-        part_copy(i)[1].wait_send()
-        return carry
-
-    lax.fori_loop(1, n_aux, sent, 0)
+    part_copy(partner).wait_send()
+    for mask in order:
+        for c in range(members):
+            part_copy(flipped(mask) * members + c).wait_send()
 
 
 def shards(integrals, densities, screen, factor, diag_inv):
@@ -828,23 +898,23 @@
 
     weights = 2 * block * block * 4 + 10 * block * block * 2
     fits = weights + integrals.size * 2 <= VMEM_ROOM
-    if breadth == block and members == 2 and n_pair == SOLVE_BLOCKS and fits:
+    if breadth == block and members == 2 and n_pair == SOLVE_BLOCKS and n_aux == 8 and fits:
         body = lead_kernel
-        screen_space = pl.ANY
+        screen_space = pltpu.HBM
         scratch = [
             pltpu.SMEM(screen.shape, screen.dtype), vmem((height, width), BF16), vmem((count, width), BF16),
             vmem((block, block), F32), vmem((block, block), F32),
             *[vmem((block, block), BF16) for _ in range(10)],
             rows(), rows(n_pair, members), whole(kind=P_KIND), whole(n_pair, members, kind=P_KIND),
-            whole(kind=U_KIND), whole(n_pair, kind=U_KIND), whole(2, kind=S_KIND), whole(kind=S_KIND),
-            whole(2, kind=BF16), whole(kind=BF16), whole(kind=V_KIND), whole(SOLVE_BLOCKS, n_pair, kind=V_KIND),
+            whole(), whole(n_pair), whole(kind=S_KIND), whole(kind=S_KIND), whole(2), whole(),
+            whole(2), whole(), whole(kind=V_KIND), whole(kind=V_KIND), whole(), whole(SOLVE_BLOCKS, n_pair),
             whole(), whole(), whole(), vmem((members, count, height), BF16),
             whole(kind=L_KIND), whole(kind=L_KIND),
             vmem((n_aux, count, share), BF16), vmem((n_aux, count, share), BF16),
-            dma((width // STREAM,)), dma((4,)),
+            dma((width // LEAD_STREAM,)), dma((4,)),
             dma, dma((members,)), dma, dma((members,)),
             dma, dma((n_pair, members)), dma((2,)), dma((n_pair, members)), dma, dma((n_pair,)),
-            dma((3,)), dma, dma((3,)), dma, dma, dma((SOLVE_BLOCKS, n_pair)),
+            dma, dma, dma((2,)), dma, dma((3,)), dma, dma, dma, dma, dma((SOLVE_BLOCKS, n_pair)),
             dma((members, n_pair)), dma, dma((members, n_pair)), dma,
             dma((n_aux,)), dma((n_aux,)),
         ]
@@ -871,16 +941,16 @@
         functools.partial(body, n_aux, n_pair),
         out_shape=jax.ShapeDtypeStruct((count, share), F32),
         in_specs=[
-            pl.BlockSpec(memory_space=pl.ANY),
-            pl.BlockSpec(memory_space=pl.ANY),
+            pl.BlockSpec(memory_space=pltpu.HBM),
+            pl.BlockSpec(memory_space=pltpu.HBM),
             pl.BlockSpec(memory_space=screen_space),
-            pl.BlockSpec(memory_space=pl.ANY),
-            pl.BlockSpec(memory_space=pl.ANY),
+            pl.BlockSpec(memory_space=pltpu.HBM),
+            pl.BlockSpec(memory_space=pltpu.HBM),
         ],
         out_specs=pl.BlockSpec(memory_space=pltpu.VMEM),
         scratch_shapes=scratch,
         compiler_params=pltpu.CompilerParams(
-            collective_id=0, has_side_effects=True, vmem_limit_bytes=60 * 2**20
+            collective_id=0, has_side_effects=True, vmem_limit_bytes=VMEM_LIMIT if body is lead_kernel else 60 * 2**20
         ),
     )(integrals, densities, screen, factor, diag_inv)
 

time: 40.6 us -> 36.1 us (0.89)
  the two profiles are of different devices: /device:TPU:12 before, /device:TPU:9 now
where the time goes in v2:
time: 36.1 us; the launch traced here: 36 us
  Pallas kernels  34.6 us (96%)
  local copies, waits for them, and re-layouts  1.31 us (4%)
    pallas_call x1, Pallas kernels, shards(): pl.pallas_call(functools.partial(body, n_aux, n_pair), out_shape=jax.Shap...  34.6 us
    unnamed x3, local copies, waits for them, and re-layouts  1.31 us

profile of v2, /device:TPU:9, one launch (start us, length us, event | category | flops | bytes accessed | tf_op | source)
XLA Modules:
  0.0 36.0 jit_solution(10590809200179614341)
XLA Ops:
  0.0 0.0 copy-start
  0.0 0.7 %copy-done = s32[3,64]{1,0:T(4,128)S(1)} copy-done((s32[3,64]{1,0:T(4,128)S(1)}, s32[3,64]{1,0:T(4,128)}, u32[]{:S(2)}) %copy-start) | copy-done | bytes 792
  0.7 34.6 %shard_map.55 = f32[16,1024]{1,0:T(8,128)S(1)} custom-call(bf16[384,8192]{1,0:T(8,128)(2,1)} %integrals.1, bf16[16,8192]{1,0:T(8,128)(2,1)} %densities.1, s32[3,64]{1,0:T(4,128)S(1)} %copy-done, f32[384,768]{1,0:T(8,128)} %factor.1, f32[384,768]{1,0:T(8,128)} %diag_inv.1), custom_call_target="tpu_custom_call" | custom-call | tf_op jit(solution)/shard_map/pallas_call | solution.py:940
  35.3 0.6 %copy.7 = f32[16,1024]{1,0:T(8,128)} copy(f32[16,1024]{1,0:T(8,128)S(1)} %shard_map.55) | data formatting | bytes 131072
Async XLA Ops:
  0.0 0.7 %copy-start = (s32[3,64]{1,0:T(4,128)S(1)}, s32[3,64]{1,0:T(4,128)}, u32[]{:S(2)}) copy-start(s32[3,64]{1,0:T(4,128)} %screen.1) | copy-start | bytes 2308

commit v3 on v2

--- a/solution.py
+++ b/solution.py
@@ -18,7 +18,7 @@
 F32 = jnp.float32
 BF16 = jnp.bfloat16
 P_KIND, S_KIND, V_KIND, L_KIND = BF16, BF16, BF16, BF16
-VMEM_LIMIT = 56400000
+VMEM_LIMIT = 44 * 2**20
 
 
 def split(values):
@@ -338,10 +338,10 @@
     integrals, densities, screen, factor, diag_inv, out,
     flags, masked, dens, fac, inv, fac_hi, fac_lo, inv_hi, inv_lo, inv_t_hi, inv_t_lo,
     step_hi, step_lo, step_t_hi, step_t_lo,
-    fit_out, fit_in, p_out, p_in, u_out, u_in, s_out, s_in, t_out, t_in, w_out, w_in, v_out, v_in, y_out, y_in,
+    fit_out, fit_in, p_out, p_in, u_out, u_in, s_out, s_in, t_out, t_in, x_out, w_out, w_in, v_out, v_in, y_out, y_in,
     resid, solved, start, rounded, last_out, last_in, part_out, part_in,
     load_sem, small_sem, fac_send, fac_recv, inv_send, inv_recv,
-    fit_send, fit_recv, p_send, p_recv, u_send, u_recv, s_send, s_recv, t_send, t_recv, w_send, w_recv,
+    fit_send, fit_recv, p_send, p_recv, u_send, u_recv, s_send, s_recv, t_send, t_recv, x_send, w_send, w_recv,
     v_send, v_recv, y_send, y_recv, round_send, round_recv, last_send, last_recv, part_send, part_recv,
 ):
     height, width = masked.shape
@@ -349,7 +349,9 @@
     count = dens.shape[0]
     members = block // height
     share = width // n_aux
-    chunks = width // LEAD_STREAM
+    chunks = width // STREAM
+    wide = LEAD_STREAM // STREAM
+    tail = chunks - wide
     strips = height // TILE
 
     row = lax.axis_index("aux")
@@ -384,7 +386,7 @@
         return remote(src, dst, send, recv, k * members + lead, z)
 
     def load(c):
-        at = pl.ds(pl.multiple_of(c * LEAD_STREAM, LEAD_STREAM), LEAD_STREAM)
+        at = pl.ds(pl.multiple_of(c * STREAM, STREAM), STREAM)
         return pltpu.make_async_copy(integrals.at[:, at], masked.at[:, at], load_sem.at[c])
 
     own = pl.ds(lead * height, height)
@@ -483,27 +485,30 @@
     def flag_of(r, t):
         return flags[r, t].astype(F32)
 
-    def fit_step(c, sums):
-        base = pl.multiple_of(c * LEAD_STREAM, LEAD_STREAM)
+    def fit_step(c, steps, sums):
+        size = steps * STREAM
+        base = pl.multiple_of(c * STREAM, STREAM)
         kept = []
         for r in range(strips):
             tiles = []
-            for t in range(LEAD_STREAM // TILE):
+            for t in range(size // TILE):
                 at = pl.ds(pl.multiple_of(base + t * TILE, TILE), TILE)
-                flag = flag_of(r, c * (LEAD_STREAM // TILE) + t)
+                flag = flag_of(r, c * (STREAM // TILE) + t)
                 tiles.append(dens[:, at] * jnp.full((count, TILE), flag, F32).astype(BF16))
             kept.append(jnp.concatenate(tiles, 1))
-        load(c).wait()
+        for i in range(steps):
+            load(c + i).wait()
         return tuple(
             sums[r] + lax.dot_general(
-                kept[r], masked[pl.ds(r * TILE, TILE), pl.ds(base, LEAD_STREAM)], NT,
+                kept[r], masked[pl.ds(r * TILE, TILE), pl.ds(base, size)], NT,
                 preferred_element_type=F32,
             )
             for r in range(strips)
         )
 
     sums = lax.fori_loop(
-        0, chunks - 1, fit_step, tuple(jnp.zeros((count, TILE), F32) for _ in range(strips))
+        0, tail // wide, lambda i, sums: fit_step(i * wide, wide, sums),
+        tuple(jnp.zeros((count, TILE), F32) for _ in range(strips)),
     )
     for c in range(members):
         @pl.when(jnp.logical_and(first, member == c))
@@ -512,7 +517,8 @@
             load_start(c).wait()
             inv_hi[own, right], inv_lo[own, right] = split(inv[own, right])
 
-    sums = fit_step(chunks - 1, sums)
+    for c in range(tail, chunks):
+        sums = fit_step(c, 1, sums)
     for r in range(strips):
         fit_out[:, pl.ds(r * TILE, TILE)] = sums[r]
 
@@ -553,15 +559,21 @@
         send_fit.start()
 
     def mask_step(c, carry):
-        base = pl.multiple_of(c * LEAD_STREAM, LEAD_STREAM)
+        base = pl.multiple_of(c * STREAM, STREAM)
         for r in range(strips):
-            for t in range(LEAD_STREAM // TILE):
-                flag = flag_of(r, c * (LEAD_STREAM // TILE) + t)
+            for t in range(STREAM // TILE):
+                flag = flag_of(r, c * (STREAM // TILE) + t)
                 at = (pl.ds(r * TILE, TILE), pl.ds(pl.multiple_of(base + t * TILE, TILE), TILE))
                 masked[at] = masked[at] * jnp.full((TILE, TILE), flag, F32).astype(BF16)
         return carry
 
     lax.fori_loop(0, chunks, mask_step, 0)
+
+    for c in range(members):
+        @pl.when(jnp.logical_and(first, member == c))
+        def _():
+            right = pl.ds(c * height, block - c * height)
+            inv_t_hi[right, :height], inv_t_lo[right, :height] = split(inv[own, right].T)
 
     @pl.when(lead_below)
     def _():
@@ -623,6 +635,9 @@
     def send_s(k, z):
         return to_lead(s_out, s_in, s_send, s_recv, k, z)
 
+    def send_x():
+        return to_lead(x_out, s_in, x_send, s_recv, 2, 0)
+
     def send_t(slot, k, z):
         return to_lead(t_out.at[slot], t_in, t_send.at[slot], t_recv, k, z)
 
@@ -635,8 +650,8 @@
     def send_y():
         return to_lead(y_out, y_in.at[mine, col], y_send, y_recv.at[mine, col], 1, 0)
 
-    def send_w(i, slot, k, z):
-        return to_lead(w_out.at[slot], w_in, w_send.at[i], w_recv, k, z)
+    def send_w(i, k, z):
+        return to_lead(w_out, w_in, w_send.at[i], w_recv, k, z)
 
     def wait_s():
         send_s(0, 0).wait_recv()
@@ -654,7 +669,7 @@
         return y_in[k, z]
 
     def wait_w():
-        send_w(0, 0, 0, 0).wait_recv()
+        send_w(0, 0, 0).wait_recv()
 
     def round_copy(k, c, i, z):
         return remote(
@@ -711,8 +726,8 @@
         u_out[...] = dot_split(start[...], step_hi[...], step_lo[...], NN)
         send_u(2).start()
         prepare_back()
-        wait_w()
-        y_out[...] = dot_split(w_in[...], step_t_hi[...], step_t_lo[...], NN)
+        wait_s()
+        y_out[...] = apply(s_in[...], step_t_hi[...], step_t_lo[...], NN)
         send_y().start()
 
     @pl.when(jnp.logical_or(role(3, 0), role(3, 1)))
@@ -749,14 +764,14 @@
         take_u(1)
         wait_s()
         solved[...] = resid[...] - apply(s_in[...], step_hi[...], step_lo[...], NN)
-        w_out[0] = solved[...]
-        send_w(0, 0, 3, 1).start()
-        send_w(1, 0, 3, 0).start()
+        w_out[...] = solved[...]
+        send_w(0, 3, 1).start()
+        send_w(1, 3, 0).start()
         back = dot_split(solved[...], step_t_hi[...], step_t_lo[...], NN)
         v_out[...] = back.astype(v_out.dtype)
         send_v(2, 1).start()
-        w_out[1] = s_in[...].astype(F32) - back
-        send_w(2, 1, 2, 0).start()
+        x_out[...] = (s_in[...].astype(F32) - back).astype(x_out.dtype)
+        send_x().start()
         coef = dot_split(solved[...], inv_t_hi[...], inv_t_lo[...], NN)
         for c in range(members):
             rounded[c] = coef[:, c * height:(c + 1) * height].astype(BF16)
@@ -773,7 +788,9 @@
             remote(
                 last_out.at[:, right], last_in.at[:, right], last_send.at[c, 0], last_recv, row, col
             ).wait_recv()
-            rounded[c] = apply(last_in[:, right], inv_hi[own, right], inv_lo[own, right], NT).astype(BF16)
+            rounded[c] = apply(
+                last_in[:, right], inv_t_hi[right, :height], inv_t_lo[right, :height], NN
+            ).astype(BF16)
 
     mine_rounded = rounded[member]
 
@@ -870,9 +887,9 @@
     @pl.when(role(3, 2))
     def _():
         send_v(2, 1).wait_send()
-        send_w(2, 1, 2, 0).wait_send()
-        send_w(0, 0, 3, 1).wait_send()
-        send_w(1, 0, 3, 0).wait_send()
+        send_x().wait_send()
+        send_w(0, 3, 1).wait_send()
+        send_w(1, 3, 0).wait_send()
         spread_rounded(3, False)
 
     part_copy(partner).wait_send()
@@ -907,14 +924,15 @@
             *[vmem((block, block), BF16) for _ in range(10)],
             rows(), rows(n_pair, members), whole(kind=P_KIND), whole(n_pair, members, kind=P_KIND),
             whole(), whole(n_pair), whole(kind=S_KIND), whole(kind=S_KIND), whole(2), whole(),
-            whole(2), whole(), whole(kind=V_KIND), whole(kind=V_KIND), whole(), whole(SOLVE_BLOCKS, n_pair),
+            whole(kind=S_KIND), whole(), whole(), whole(kind=V_KIND), whole(kind=V_KIND),
+            whole(), whole(SOLVE_BLOCKS, n_pair),
             whole(), whole(), whole(), vmem((members, count, height), BF16),
             whole(kind=L_KIND), whole(kind=L_KIND),
             vmem((n_aux, count, share), BF16), vmem((n_aux, count, share), BF16),
-            dma((width // LEAD_STREAM,)), dma((4,)),
+            dma((width // STREAM,)), dma((4,)),
             dma, dma((members,)), dma, dma((members,)),
             dma, dma((n_pair, members)), dma((2,)), dma((n_pair, members)), dma, dma((n_pair,)),
-            dma, dma, dma((2,)), dma, dma((3,)), dma, dma, dma, dma, dma((SOLVE_BLOCKS, n_pair)),
+            dma, dma, dma((2,)), dma, dma, dma((2,)), dma, dma, dma, dma, dma((SOLVE_BLOCKS, n_pair)),
             dma((members, n_pair)), dma, dma((members, n_pair)), dma,
             dma((n_aux,)), dma((n_aux,)),
         ]
@@ -937,6 +955,9 @@
             dma((n_pair,)), dma, dma((pieces, members)), dma((n_aux, members)),
             dma((n_aux,)), dma((n_aux,)),
         ]
+    operands = integrals, densities, screen, factor, diag_inv
+    if body is lead_kernel:
+        operands = tuple(pltpu.with_memory_space_constraint(x, pltpu.HBM) for x in operands)
     return pl.pallas_call(
         functools.partial(body, n_aux, n_pair),
         out_shape=jax.ShapeDtypeStruct((count, share), F32),
@@ -952,7 +973,7 @@
         compiler_params=pltpu.CompilerParams(
             collective_id=0, has_side_effects=True, vmem_limit_bytes=VMEM_LIMIT if body is lead_kernel else 60 * 2**20
         ),
-    )(integrals, densities, screen, factor, diag_inv)
+    )(*operands)
 
 
 def solution(mesh):

time: 36.1 us -> 35.7 us (0.989)
  local copies, waits for them, and re-layouts: 1.31 us -> 0.63 us
    unnamed x3 -> x1, local copies, waits for them, and re-layouts: 1.31 us -> 0.63 us
where the time goes in v3:
time: 35.7 us; the launch traced here: 35.6 us
  Pallas kernels  34.9 us (98%)
  local copies, waits for them, and re-layouts  0.63 us (2%)
    pallas_call x1, Pallas kernels, shards(): pl.pallas_call(functools.partial(body, n_aux, n_pair), out_shape=jax.Shap...  34.9 us

profile of v3, /device:TPU:9, one launch (start us, length us, event | category | flops | bytes accessed | tf_op | source)
XLA Modules:
  0.0 35.6 jit_solution(6441112839376003596)
XLA Ops:
  0.0 34.9 %shard_map.55 = f32[16,1024]{1,0:T(8,128)S(1)} custom-call(bf16[384,8192]{1,0:T(8,128)(2,1)} %integrals.1, bf16[16,8192]{1,0:T(8,128)(2,1)} %densities.1, s32[3,64]{1,0:T(4,128)} %screen.1, f32[384,768]{1,0:T(8,128)} %factor.1, f32[384,768]{1,0:T(8,128)} %diag_inv.1), custom_call_target="tpu_custom_call" | custom-call | tf_op jit(solution)/shard_map/pallas_call | solution.py:961
  34.9 0.6 %copy.7 = f32[16,1024]{1,0:T(8,128)} copy(f32[16,1024]{1,0:T(8,128)S(1)} %shard_map.55) | data formatting | bytes 131072

commit v4 on v3

--- a/solution.py
+++ b/solution.py
@@ -339,10 +339,10 @@
     flags, masked, dens, fac, inv, fac_hi, fac_lo, inv_hi, inv_lo, inv_t_hi, inv_t_lo,
     step_hi, step_lo, step_t_hi, step_t_lo,
     fit_out, fit_in, p_out, p_in, u_out, u_in, s_out, s_in, t_out, t_in, x_out, w_out, w_in, v_out, v_in, y_out, y_in,
-    resid, solved, start, rounded, last_out, last_in, part_out, part_in,
+    resid, solved, start, rounded, last_out, last_in, pair_out, pair_in, part_out, part_in,
     load_sem, small_sem, fac_send, fac_recv, inv_send, inv_recv,
     fit_send, fit_recv, p_send, p_recv, u_send, u_recv, s_send, s_recv, t_send, t_recv, x_send, w_send, w_recv,
-    v_send, v_recv, y_send, y_recv, round_send, round_recv, last_send, last_recv, part_send, part_recv,
+    v_send, v_recv, y_send, y_recv, round_send, round_recv, last_send, last_recv, pair_send, pair_recv, part_send, part_recv,
 ):
     height, width = masked.shape
     block = inv.shape[1]
@@ -816,27 +816,40 @@
             part_out.at[target], part_in.at[row], part_send.at[target], part_recv.at[row], target, col
         )
 
-    for mask in order:
+    def halves_of(values):
+        left, right = values[:, :share], values[:, share:]
+        return jnp.where(member == 0, left, right), jnp.where(member == 0, right, left)
+
+    far, near = flipped(order[0]), order[1:]
+    far_copy = part_copy(far * members + member)
+    pair_copy = remote(pair_out, pair_in, pair_send, pair_recv, partner, col)
+
+    far_own, far_other = halves_of(product(far))
+    pair_out[...] = far_other
+    pair_copy.start()
+    for mask in near:
         group = flipped(mask)
         values = product(group)
         for c in range(members):
             part_out[group * members + c] = values[:, c * share:(c + 1) * share].astype(BF16)
             part_copy(group * members + c).start()
 
-    values = product(mine)
-    halves = values[:, :share], values[:, share:]
-    part_out[partner] = jnp.where(member == 0, halves[1], halves[0]).astype(BF16)
+    total, other = halves_of(product(mine))
+    part_out[partner] = other.astype(BF16)
     part_copy(partner).start()
-    total = jnp.where(member == 0, halves[0], halves[1])
+    pair_copy.wait_recv()
+    part_out[far * members + member] = (far_own + pair_in[...]).astype(BF16)
+    far_copy.start()
 
     def take(source):
         remote(part_out.at[0], part_in.at[source], part_send.at[0], part_recv.at[source], row, col).wait_recv()
         return part_in[source].astype(F32)
 
     total += take(partner)
-    for mask in reversed(order):
+    for mask in near:
         for c in range(members):
             total += take(flipped(mask) * members + c)
+    total += take(far * members + member)
 
     out[...] = total
 
@@ -892,8 +905,10 @@
         send_w(1, 3, 0).wait_send()
         spread_rounded(3, False)
 
+    pair_copy.wait_send()
+    far_copy.wait_send()
     part_copy(partner).wait_send()
-    for mask in order:
+    for mask in near:
         for c in range(members):
             part_copy(flipped(mask) * members + c).wait_send()
 
@@ -927,13 +942,13 @@
             whole(kind=S_KIND), whole(), whole(), whole(kind=V_KIND), whole(kind=V_KIND),
             whole(), whole(SOLVE_BLOCKS, n_pair),
             whole(), whole(), whole(), vmem((members, count, height), BF16),
-            whole(kind=L_KIND), whole(kind=L_KIND),
+            whole(kind=L_KIND), whole(kind=L_KIND), vmem((count, share), F32), vmem((count, share), F32),
             vmem((n_aux, count, share), BF16), vmem((n_aux, count, share), BF16),
             dma((width // STREAM,)), dma((4,)),
             dma, dma((members,)), dma, dma((members,)),
             dma, dma((n_pair, members)), dma((2,)), dma((n_pair, members)), dma, dma((n_pair,)),
             dma, dma, dma((2,)), dma, dma, dma((2,)), dma, dma, dma, dma, dma((SOLVE_BLOCKS, n_pair)),
-            dma((members, n_pair)), dma, dma((members, n_pair)), dma,
+            dma((members, n_pair)), dma, dma((members, n_pair)), dma, dma, dma,
             dma((n_aux,)), dma((n_aux,)),
         ]
     else:

time: 35.7 us -> 35.3 us (0.989)
  Pallas kernels: 34.9 us -> 34.2 us
    pallas_call x1, Pallas kernels: 34.9 us -> 34.2 us  [shards(): pl.pallas_call(functools.partial(body, n_aux, n_pair), out_shape=jax.Shap...]
where the time goes in v4:
time: 35.3 us; the launch traced here: 34.9 us
  Pallas kernels  34.2 us (97%)
  local copies, waits for them, and re-layouts  0.63 us (2%)
    pallas_call x1, Pallas kernels, shards(): pl.pallas_call(functools.partial(body, n_aux, n_pair), out_shape=jax.Shap...  34.2 us

profile of v4, /device:TPU:9, one launch (start us, length us, event | category | flops | bytes accessed | tf_op | source)
XLA Modules:
  0.0 34.9 jit_solution(17189314778363019416)
XLA Ops:
  0.0 34.2 %shard_map.55 = f32[16,1024]{1,0:T(8,128)S(1)} custom-call(bf16[384,8192]{1,0:T(8,128)(2,1)} %integrals.1, bf16[16,8192]{1,0:T(8,128)(2,1)} %densities.1, s32[3,64]{1,0:T(4,128)} %screen.1, f32[384,768]{1,0:T(8,128)} %factor.1, f32[384,768]{1,0:T(8,128)} %diag_inv.1), custom_call_target="tpu_custom_call" | custom-call | tf_op jit(solution)/shard_map/pallas_call | solution.py:976
  34.2 0.6 %copy.7 = f32[16,1024]{1,0:T(8,128)} copy(f32[16,1024]{1,0:T(8,128)S(1)} %shard_map.55) | data formatting | bytes 131072

commit v5 on v4

--- a/solution.py
+++ b/solution.py
@@ -517,8 +517,7 @@
             load_start(c).wait()
             inv_hi[own, right], inv_lo[own, right] = split(inv[own, right])
 
-    for c in range(tail, chunks):
-        sums = fit_step(c, 1, sums)
+    sums = fit_step(tail, wide, sums)
     for r in range(strips):
         fit_out[:, pl.ds(r * TILE, TILE)] = sums[r]
 

time: 35.3 us -> 35.2 us (level)
  no operation moved by 1% of the time
where the time goes in v5:
time: 35.2 us; the launch traced here: 34.7 us
  Pallas kernels  34.1 us (97%)
  local copies, waits for them, and re-layouts  0.63 us (2%)
    pallas_call x1, Pallas kernels, shards(): pl.pallas_call(functools.partial(body, n_aux, n_pair), out_shape=jax.Shap...  34.1 us

profile of v5, /device:TPU:9, one launch (start us, length us, event | category | flops | bytes accessed | tf_op | source)
XLA Modules:
  0.0 34.7 jit_solution(16451949641152251260)
XLA Ops:
  0.0 34.1 %shard_map.55 = f32[16,1024]{1,0:T(8,128)S(1)} custom-call(bf16[384,8192]{1,0:T(8,128)(2,1)} %integrals.1, bf16[16,8192]{1,0:T(8,128)(2,1)} %densities.1, s32[3,64]{1,0:T(4,128)} %screen.1, f32[384,768]{1,0:T(8,128)} %factor.1, f32[384,768]{1,0:T(8,128)} %diag_inv.1), custom_call_target="tpu_custom_call" | custom-call | tf_op jit(solution)/shard_map/pallas_call | solution.py:975
  34.1 0.6 %copy.7 = f32[16,1024]{1,0:T(8,128)} copy(f32[16,1024]{1,0:T(8,128)S(1)} %shard_map.55) | data formatting | bytes 131072
